TPU v7x, 32 devices: a 4x2x2 block of a 4x4x8 slice. The times are simulated.
32 devices in a mesh: bs: 4 (over y, z), tp: 8 (over x, core).
Axes of the slice: x: 4, y: 2, z: 2, core: 2. Of those that a mesh axis runs over, the one named last changes fastest.
The devices are a block of a 4x4x8 slice.
Arguments:
- new_hidden: bfloat16 [512, 3072], P('bs'), parts along dimension 0
- cache_k: bfloat16 [512, 64, 8, 128], P('bs', None, 'tp'), parts along dimension 0
- cache_v: bfloat16 [512, 64, 8, 128], P('bs', None, 'tp'), parts along dimension 0
- lengths: int32 [512], P('bs'), parts along dimension 0
- ln1_gain: float32 [3072], replicated
- ln1_bias: float32 [3072], replicated
- w_q: bfloat16 [3072, 3072], P(None, 'tp')
- w_k: bfloat16 [3072, 1024], P(None, 'tp')
- w_v: bfloat16 [3072, 1024], P(None, 'tp')
- w_o: bfloat16 [3072, 3072], P('tp')
- ln2_gain: float32 [3072], replicated
- ln2_bias: float32 [3072], replicated
- w_up: bfloat16 [3072, 8192], P(None, 'tp')
- w_down: bfloat16 [8192, 3072], P('tp')
- lnf_gain: float32 [3072], replicated
- lnf_bias: float32 [3072], replicated
- w_out: bfloat16 [3072, 128256], P(None, 'tp')
Outputs:
- output 1: float32 [512, 128256], P('bs', 'tp'), parts along dimension 0
- output 2: bfloat16 [512, 64, 8, 128], P('bs', None, 'tp'), parts along dimension 0
- output 3: bfloat16 [512, 64, 8, 128], P('bs', None, 'tp'), parts along dimension 0
- output 4: bfloat16 [512, 3072], P('bs'), parts along dimension 0
There are 4 independent parts. A program takes and returns all parts, laid end to end along the dimension named above; an argument that names none is the same for every part.
All inputs are finite; a program needn't handle non-finite values.
Results may differ from a plain program's by a relative error of at most 0.0124614.
Values are sent between devices in bfloat16 or wider.
A program may use at most 768 MiB of HBM per device.

v0:
```python
import jax
import jax.numpy as jnp
from jax import lax
from jax.sharding import PartitionSpec as P

EPSILON = 1e-5
ROPE_BASE = 10000.0


def layer_norm1p(values, gain, bias):
    mean = jnp.mean(values, axis=-1, keepdims=True)
    centered = values - mean
    variance = jnp.mean(jnp.square(centered), axis=-1, keepdims=True)
    return centered * lax.rsqrt(variance + EPSILON) * (1.0 + gain) + bias


def apply_rotary(vecs, positions):
    rot_dim = vecs.shape[-1] // 2
    half_rot = rot_dim // 2
    exponent = -2.0 * jnp.arange(half_rot, dtype=jnp.float32) / rot_dim
    inv_freq = ROPE_BASE ** exponent
    angles = positions.astype(jnp.float32)[:, None] * inv_freq[None, :]
    cosine = jnp.cos(angles)[:, None, :]
    sine = jnp.sin(angles)[:, None, :]
    first = vecs[..., :half_rot]
    second = vecs[..., half_rot:rot_dim]
    return jnp.concatenate([first * cosine - second * sine, second * cosine + first * sine, vecs[..., rot_dim:]], axis=-1)


def project_and_attend(new_hidden, cache_k, cache_v, lengths, ln1_gain, ln1_bias, w_q, w_k, w_v):
    batch, cache_len, kv_heads, head_dim = cache_k.shape
    normed = layer_norm1p(new_hidden.astype(jnp.float32), ln1_gain, ln1_bias).astype(jnp.bfloat16)
    query = jnp.dot(normed, w_q, preferred_element_type=jnp.float32).reshape(batch, -1, head_dim)
    key_new = jnp.dot(normed, w_k, preferred_element_type=jnp.float32).reshape(batch, kv_heads, head_dim)
    val_new = jnp.dot(normed, w_v, preferred_element_type=jnp.float32).reshape(batch, kv_heads, head_dim)
    query = apply_rotary(query, lengths).astype(jnp.bfloat16)
    key_new = apply_rotary(key_new, lengths).astype(jnp.bfloat16)
    val_new = val_new.astype(jnp.bfloat16)
    positions = jnp.arange(cache_len)
    write_slot = (positions[None, :] == lengths[:, None])[:, :, None, None]
    new_cache_k = jnp.where(write_slot, key_new[:, None], cache_k)
    new_cache_v = jnp.where(write_slot, val_new[:, None], cache_v)
    group = query.shape[1] // kv_heads
    q_groups = query.reshape(batch, kv_heads, group, head_dim)
    score_scale = head_dim ** -0.5
    scores = jnp.einsum('bgrk,blgk->bgrl', q_groups, new_cache_k, preferred_element_type=jnp.float32) * score_scale
    valid = (positions[None, :] <= lengths[:, None])[:, None, None, :]
    scores = jnp.where(valid, scores, -1e30)
    attn_prob = jax.nn.softmax(scores, axis=-1).astype(jnp.bfloat16)
    mixed = jnp.einsum('bgrl,blgk->bgrk', attn_prob, new_cache_v, preferred_element_type=jnp.float32)
    return mixed.astype(jnp.bfloat16).reshape(batch, -1), new_cache_k, new_cache_v


def reduce_to_all(partial, residual, ways):
    batch, width = partial.shape
    piece = width // ways
    received = lax.all_to_all(partial, 'tp', 1, 0, tiled=True)
    summed = jnp.sum(received.reshape(ways, batch, piece).astype(jnp.float32), axis=0)
    start = lax.axis_index('tp') * piece
    own_resid = lax.dynamic_slice_in_dim(residual, start, piece, axis=1)
    own_sum = (own_resid.astype(jnp.float32) + summed).astype(jnp.bfloat16)
    return lax.all_gather(own_sum, 'tp', axis=1, tiled=True)


def solution(mesh):
    ways = mesh.shape['tp']
    row_spec = P('bs', None)
    cache_spec = P('bs', None, 'tp', None)
    col_split = P(None, 'tp')
    row_split = P('tp', None)
    in_specs = (row_spec, cache_spec, cache_spec, P('bs'), P(), P(), col_split, col_split, col_split, row_split, P(), P(), col_split, row_split, P(), P(), col_split)
    out_specs = (P('bs', 'tp'), cache_spec, cache_spec, row_spec)

    def local_step(new_hidden, cache_k, cache_v, lengths, ln1_gain, ln1_bias, w_q, w_k, w_v, w_o, ln2_gain, ln2_bias, w_up, w_down, lnf_gain, lnf_bias, w_out):
        attended, new_cache_k, new_cache_v = project_and_attend(new_hidden, cache_k, cache_v, lengths, ln1_gain, ln1_bias, w_q, w_k, w_v)
        partial_o = jnp.dot(attended, w_o, preferred_element_type=jnp.float32).astype(jnp.bfloat16)
        mid_hidden = reduce_to_all(partial_o, new_hidden, ways)
        normed_mid = layer_norm1p(mid_hidden.astype(jnp.float32), ln2_gain, ln2_bias).astype(jnp.bfloat16)
        up_proj = jnp.dot(normed_mid, w_up, preferred_element_type=jnp.float32)
        activated = jnp.square(jnp.maximum(up_proj, 0.0)).astype(jnp.bfloat16)
        partial_m = jnp.dot(activated, w_down, preferred_element_type=jnp.float32).astype(jnp.bfloat16)
        out_hidden = reduce_to_all(partial_m, mid_hidden, ways)
        normed_out = layer_norm1p(out_hidden.astype(jnp.float32), lnf_gain, lnf_bias).astype(jnp.bfloat16)
        logits = jnp.dot(normed_out, w_out, preferred_element_type=jnp.float32)
        local_peak = jnp.max(logits, axis=-1)
        local_total = jnp.sum(jnp.exp(logits - local_peak[:, None]), axis=-1)
        gathered = lax.all_gather(jnp.stack([local_peak, local_total]), 'tp')
        global_peak = jnp.max(gathered[:, 0], axis=0)
        global_total = jnp.sum(gathered[:, 1] * jnp.exp(gathered[:, 0] - global_peak[None, :]), axis=0)
        log_probs = logits - (global_peak + jnp.log(global_total))[:, None]
        return log_probs, new_cache_k, new_cache_v, out_hidden

    return jax.shard_map(local_step, mesh=mesh, in_specs=in_specs, out_specs=out_specs, check_vma=False)
```

profile of v0, /device:TPU:81, one launch (start us, length us, event | category | flops | bytes accessed | tf_op | source)
XLA Modules:
  0.0 159.7 jit_solution(2243467799438566496)
XLA Ops:
  0.6 0.0 copy-start
  0.6 0.0 copy-start.2
  0.7 0.8 convert_element_type.76
  1.5 1.4 iota_compare_fusion.1
  3.0 1.3 convert_reduce_fusion.2
  4.3 1.5 fusion.19
  5.8 0.6 convolution_bitcast_fusion
  6.5 0.1 fusion.62
  6.6 1.0 multiply_cosine_fusion
  7.6 1.2 fusion.66
  8.8 0.6 fusion.68
  9.4 1.1 convolution_convert_fusion.2
  10.5 0.7 copy.43
  11.3 0.8 copy.53
  12.0 0.1 copy.52
  12.1 0.9 copy.51
  13.1 0.9 subtract_convert_fusion
  14.0 1.0 pad_maximum_fusion
  15.0 4.8 %broadcast_select_fusion.1 = (bf16[128,64,1,128]{3,1,2,0:T(8,128)(2,1)S(1)}, bf16[128,64,1,128]{3,1,2,0:T(8,128)(2,1)}) fusion(bf16[128,64,1,128]{3,1,2,0:T(8,128)(2,1)} %param.18, pred[128,64]{1,0:T(8,128)(4,1)} %get-tuple-element.18, bf16[128,128]{1,0:T(8,128)(2,1)} %copy.43, bf16[128,64,1,128]{3,1,2,0:T(8,128)(2,1)} %param.19, ...), kind=kLoop, calls=%fused_computation.10 | loop fusion | flops 2097152 | bytes 8462336 | tf_op jit(solution)/shard_map/jit(_where)/select_n | solution.py:41
  19.8 1.3 copy-done.1
  21.1 1.2 fusion.29
  22.3 1.0 fusion.70
  23.3 3.5 %fusion.33 = bf16[128,3,128]{2,1,0:T(4,128)(2,1)S(1)} fusion(bf16[128,64,1,128]{3,1,2,0:T(8,128)(2,1)} %get-tuple-element.27, f32[128,3]{1,0:T(8,128)} %fusion.70, f32[128,3,64]{2,1,0:T(4,128)S(1)} %fusion.29), kind=kOutput, calls=%fused_computation.44 | convolution fusion | flops 6414783 | bytes 2295296 | tf_op jit(solution)/shard_map/bgrl,blgk->bgrk/dot_general | solution.py:50
  26.8 0.1 copy.45
  27.0 0.6 convolution_convert_fusion.1
  27.6 0.0 copy-start.6
  27.6 1.0 copy.61
  28.6 6.1 %all-to-all-start = ((bf16[128,8,384]{2,0,1:T(8,128)(2,1)}), bf16[128,8,384]{2,0,1:T(8,128)(2,1)}, u32[]{:S(2)}, u32[]{:S(2)}) async-start(bf16[128,8,384]{2,0,1:T(8,128)(2,1)} %bitcast.48), calls=%async_computation | async-start | bytes 1572864 | tf_op jit(solution)/shard_map/all_to_all | solution.py:57
  34.7 12.1 %all-to-all-done = bf16[128,8,384]{2,0,1:T(8,128)(2,1)} async-done(((bf16[128,8,384]{2,0,1:T(8,128)(2,1)}), bf16[128,8,384]{2,0,1:T(8,128)(2,1)}, u32[]{:S(2)}, u32[]{:S(2)}) %all-to-all-start) | async-done | bytes 786464 | tf_op jit(solution)/shard_map/all_to_all | solution.py:57
  46.8 1.3 convert_reduce_fusion.4
  48.1 0.0 copy-start.3
  48.1 14.7 %all_gather.12 = bf16[128,3072]{1,0:T(8,128)(2,1)S(1)} all-gather(bf16[128,384]{1,0:T(8,128)(2,1)S(1)} %add_convert_fusion.1), channel_id=1, replica_groups=mesh['bs'=4,'tp'=8] {'tp'}, dimensions={1}, use_global_device_ids=true | all-gather | bytes 884736 | tf_op jit(solution)/shard_map/all_gather | solution.py:62
  62.8 0.2 convert_reduce_fusion.1
  63.0 0.4 fusion.15
  63.4 7.4 %convolution_convert_fusion = bf16[128,3072]{1,0:T(8,128)(2,1)} fusion(bf16[1024,3072]{1,0:T(8,128)(2,1)} %param.30, bf16[3072,1024]{1,0:T(8,128)(2,1)} %param.29, bf16[128,3072]{1,0:T(8,128)(2,1)S(1)} %all_gather.12, f32[3072]{0:T(1024)S(1)} %copy-done.3, f32[3072]{0:T(1024)S(1)} %broadcast_add_fusion.1, f32[128]{0:T(128)S(1)} %add_rsqrt_fusion.1, ...), kind=kOutput, calls=%fused_computation.3 | convolution fusion | flops 1613758464 | bytes 14181376 | tf_op jit(solution)/shard_map/dot_general | solution.py:81
  70.8 2.1 %copy.60 = bf16[16,8,8,384]{3,2,0,1:T(8,128)(2,1)} copy(bf16[16,8,8,384]{3,2,1,0:T(8,128)(2,1)} %bitcast.51) | data formatting | bytes 1572864 | tf_op jit(solution)/shard_map/all_to_all | solution.py:57
  72.9 4.3 %all-to-all-start.1 = ((bf16[128,8,384]{2,0,1:T(8,128)(2,1)}), bf16[128,8,384]{2,0,1:T(8,128)(2,1)}, u32[]{:S(2)}, u32[]{:S(2)}) async-start(bf16[128,8,384]{2,0,1:T(8,128)(2,1)} %bitcast.49), calls=%async_computation.1 | async-start | bytes 1572864 | tf_op jit(solution)/shard_map/all_to_all | solution.py:57
  77.2 12.1 %all-to-all-done.1 = bf16[128,8,384]{2,0,1:T(8,128)(2,1)} async-done(((bf16[128,8,384]{2,0,1:T(8,128)(2,1)}), bf16[128,8,384]{2,0,1:T(8,128)(2,1)}, u32[]{:S(2)}, u32[]{:S(2)}) %all-to-all-start.1) | async-done | bytes 786464 | tf_op jit(solution)/shard_map/all_to_all | solution.py:57
  89.3 1.3 convert_reduce_fusion.3
  90.6 0.0 copy-start.4
  90.6 14.9 %all_gather.13 = bf16[128,3072]{1,0:T(8,128)(2,1)S(1)} all-gather(bf16[128,384]{1,0:T(8,128)(2,1)S(1)} %add_convert_fusion), channel_id=1, replica_groups=mesh['bs'=4,'tp'=8] {'tp'}, dimensions={1}, use_global_device_ids=true | all-gather | bytes 884736 | tf_op jit(solution)/shard_map/all_gather | solution.py:62
  105.5 0.2 convert_reduce_fusion
  105.7 0.4 fusion.11
  106.1 38.0 %fusion.71 = (f32[128]{0:T(128)S(1)}, f32[128,16032]{0,1:T(8,128)S(1)}) fusion(bf16[3072,16032]{0,1:T(8,128)(2,1)} %param.33, bf16[128,3072]{1,0:T(8,128)(2,1)S(1)} %all_gather.13, f32[3072]{0:T(1024)S(1)} %copy-done.4, f32[3072]{0:T(1024)S(1)} %broadcast_add_fusion, f32[128]{0:T(128)S(1)} %add_rsqrt_fusion, f32[128]{0:T(128)S(1)} %broadcast_multiply_fusion), kind=kOutput, calls=%fused_computation.105 | convolution fusion | flops 12612489216 | bytes 107521536 | tf_op jit(solution)/shard_map/dot_general | solution.py:84
  144.1 2.2 %exponential_reduce_fusion = f32[128]{0:T(128)S(1)} fusion(f32[128,16032]{0,1:T(8,128)S(1)} %get-tuple-element.20, f32[128]{0:T(128)S(1)} %get-tuple-element.19), kind=kLoop, calls=%fused_computation.1 | loop fusion | flops 4104064 | bytes 8209408 | tf_op jit(solution)/shard_map/reduce_sum | solution.py:86
  146.3 8.9 %all-gather.1 = f32[8,2,128]{2,1,0:T(2,128)S(1)} all-gather(f32[1,2,128]{2,1,0:T(2,128)S(1)} %maximum_bitcast_fusion), channel_id=2, replica_groups=mesh['bs'=4,'tp'=8] {'tp'}, dimensions={0}, use_global_device_ids=true | all-gather | bytes 9216 | tf_op jit(solution)/shard_map/all_gather | solution.py:87
  155.2 3.6 %broadcast_subtract_fusion = f32[128,16032]{0,1:T(8,128)} fusion(f32[128,16032]{0,1:T(8,128)S(1)} %get-tuple-element.20, f32[128]{0:T(128)S(1)} %log_add_fusion), kind=kLoop, calls=%fused_computation.2 | loop fusion | flops 2052096 | bytes 16417280 | tf_op jit(solution)/shard_map/sub | solution.py:90
  158.8 0.9 copy.63
  (37 shorter events, 0.3 us)
Async XLA Ops:
  0.6 26.3 %copy-start = (bf16[384,3072]{1,0:T(8,128)(2,1)S(1)}, bf16[384,3072]{1,0:T(8,128)(2,1)}, u32[]{:S(2)}) copy-start(bf16[384,3072]{1,0:T(8,128)(2,1)} %param.26) | copy-start | bytes 7077892
  0.6 5.2 %copy-start.2 = (bf16[128,3072]{1,0:T(8,128)(2,1)S(1)}, bf16[128,3072]{1,0:T(8,128)(2,1)}, u32[]{:S(2)}) copy-start(bf16[128,3072]{1,0:T(8,128)(2,1)} %param.17) | copy-start | bytes 2359300
  0.7 5.1 %copy-start.5 = (f32[3072]{0:T(1024)S(1)}, f32[3072]{0:T(1024)}, u32[]{:S(2)}) copy-start(f32[3072]{0:T(1024)} %param.21) | copy-start | bytes 36868
  0.7 5.2 %copy-start.11 = (f32[3072]{0:T(1024)S(1)}, f32[3072]{0:T(1024)}, u32[]{:S(2)}) copy-start(f32[3072]{0:T(1024)} %param.22) | copy-start | bytes 36868
  0.7 5.2 %copy-start.9 = (bf16[3072,128]{1,0:T(8,128)(2,1)S(1)}, bf16[3072,128]{1,0:T(8,128)(2,1)}, u32[]{:S(2)}) copy-start(bf16[3072,128]{1,0:T(8,128)(2,1)} %param.24) | copy-start | bytes 2359300
  5.8 1.8 %copy-start.8 = (bf16[3072,384]{1,0:T(8,128)(2,1)S(1)}, bf16[3072,384]{1,0:T(8,128)(2,1)}, u32[]{:S(2)}) copy-start(bf16[3072,384]{1,0:T(8,128)(2,1)} %param.23) | copy-start | bytes 7077892
  7.6 1.8 %copy-start.10 = (bf16[3072,128]{1,0:T(8,128)(2,1)S(1)}, bf16[3072,128]{1,0:T(8,128)(2,1)}, u32[]{:S(2)}) copy-start(bf16[3072,128]{1,0:T(8,128)(2,1)} %param.25) | copy-start | bytes 2359300
  19.8 1.3 copy-start.1
  27.6 7.1 %copy-start.6 = (f32[3072]{0:T(1024)S(1)}, f32[3072]{0:T(1024)}, u32[]{:S(2)}) copy-start(f32[3072]{0:T(1024)} %param.27) | copy-start | bytes 36868
  28.6 18.3 %all-to-all-start = ((bf16[128,8,384]{2,0,1:T(8,128)(2,1)}), bf16[128,8,384]{2,0,1:T(8,128)(2,1)}, u32[]{:S(2)}, u32[]{:S(2)}) async-start(bf16[128,8,384]{2,0,1:T(8,128)(2,1)} %bitcast.48), calls=%async_computation | async-start | bytes 1572864 | tf_op jit(solution)/shard_map/all_to_all | solution.py:57
  48.1 15.3 %copy-start.3 = (f32[3072]{0:T(1024)S(1)}, f32[3072]{0:T(1024)}, u32[]{:S(2)}) copy-start(f32[3072]{0:T(1024)} %param.28) | copy-start | bytes 36868
  70.8 6.4 %copy-start.7 = (f32[3072]{0:T(1024)S(1)}, f32[3072]{0:T(1024)}, u32[]{:S(2)}) copy-start(f32[3072]{0:T(1024)} %param.31) | copy-start | bytes 36868
  72.9 16.4 %all-to-all-start.1 = ((bf16[128,8,384]{2,0,1:T(8,128)(2,1)}), bf16[128,8,384]{2,0,1:T(8,128)(2,1)}, u32[]{:S(2)}, u32[]{:S(2)}) async-start(bf16[128,8,384]{2,0,1:T(8,128)(2,1)} %bitcast.49), calls=%async_computation.1 | async-start | bytes 1572864 | tf_op jit(solution)/shard_map/all_to_all | solution.py:57
  90.6 15.5 %copy-start.4 = (f32[3072]{0:T(1024)S(1)}, f32[3072]{0:T(1024)}, u32[]{:S(2)}) copy-start(f32[3072]{0:T(1024)} %param.32) | copy-start | bytes 36868
where the time goes:
time: 161 us; the launch traced here: 160 us
  matrix products  53.6 us (33%)
  blocking collectives  38.4 us (24%)
  waiting for transfers between devices  24.2 us (15%)
  other arithmetic  23.5 us (15%)
  starting transfers between devices  10.4 us (6%)
  local copies, waits for them, and re-layouts  8.64 us (5%)
    dot_general x1, matrix products, local_step(): logits = jnp.dot(normed_out, w_out, preferred_element_type=jnp.float32)  38 us
    all_gather x2, blocking collectives, reduce_to_all(): return lax.all_gather(own_sum, 'tp', axis=1, tiled=True)  29.6 us
    all_to_all x2, waiting for transfers between devices, reduce_to_all(): received = lax.all_to_all(partial, 'tp', 1, 0, tiled=True)  24.2 us
    all_to_all x2, starting transfers between devices, reduce_to_all(): received = lax.all_to_all(partial, 'tp', 1, 0, tiled=True)  10.4 us
    all_gather x1, blocking collectives, local_step(): gathered = lax.all_gather(jnp.stack([local_peak, local_total]), 'tp')  8.87 us
    dot_general x1, matrix products, local_step(): jnp.dot(activated, w_down, preferred_element_type=jnp.float32)  7.4 us
    select_n x1, other arithmetic, project_and_attend(): new_cache_k = jnp.where(write_slot, key_new[:, None], cache_k)  4.77 us
    unnamed x28, local copies, waits for them, and re-layouts  4.06 us
  transfers between devices with their start and end apart: 2, of which 2 were waited for; matrix products, arithmetic and copies ran while one was open for 0% of the time, Pallas kernels for 0%

commit v1 on v0

--- a/solution.py
+++ b/solution.py
@@ -1,10 +1,20 @@
+import functools
+
 import jax
 import jax.numpy as jnp
 from jax import lax
+from jax.experimental import pallas as pl
+from jax.experimental.pallas import tpu as pltpu
 from jax.sharding import PartitionSpec as P
 
 EPSILON = 1e-5
 ROPE_BASE = 10000.0
+BF16 = jnp.bfloat16
+F32 = jnp.float32
+MESH = pl.DeviceIdType.MESH
+RING = 14
+ROWS = 512
+NSEM = 26
 
 
 def layer_norm1p(values, gain, bias):
@@ -51,15 +61,330 @@
     return mixed.astype(jnp.bfloat16).reshape(batch, -1), new_cache_k, new_cache_v
 
 
-def reduce_to_all(partial, residual, ways):
-    batch, width = partial.shape
+def dotf(lhs, rhs):
+    return jnp.dot(lhs, rhs, preferred_element_type=F32)
+
+
+def fold(values):
+    out = values[:, 0:128]
+    for lane in range(128, values.shape[1], 128):
+        out = out + values[:, lane:lane + 128]
+    return out
+
+
+def norm_chunks(chunks, gain, bias, out):
+    count, rows, piece = chunks.shape
+    width = count * piece
+    total = jnp.zeros((rows, 128), F32)
+    for j in range(count):
+        total = total + fold(chunks[j].astype(F32))
+    mean = jnp.sum(total, axis=-1, keepdims=True) / width
+    total = jnp.zeros((rows, 128), F32)
+    for j in range(count):
+        total = total + fold(jnp.square(chunks[j].astype(F32) - mean))
+    scale = lax.rsqrt(jnp.sum(total, axis=-1, keepdims=True) / width + EPSILON)
+    for j in range(count):
+        cols = slice(j * piece, (j + 1) * piece)
+        normed = (chunks[j].astype(F32) - mean) * scale * (1.0 + gain[:, cols]) + bias[:, cols]
+        out[:, cols] = normed.astype(BF16)
+
+
+def tail_kernel(ways, attended, hidden, w_o, w_up, w_down, w_out, gain2, bias2, gainf, biasf,
+                logits, norm_out, y_out,
+                ring, last, resid, act, normed, normed_t, parts, raw1, raw2, sib, sibh, send3, recv3, own, gath, stats,
+                w_sem, small_sem, send_sem, recv_sem, stat_send, stat_recv):
+    me = lax.axis_index('tp')
+    core = lax.rem(me, 2)
+    chip = me // 2
+    chips = ways // 2
+    right = lax.rem(chip + 1, chips)
+    left = lax.rem(chip + chips - 1, chips)
+    far = lax.rem(chip + 2, chips)
+    other = 1 - core
+    rows, piece = resid.shape
+    half = rows // 2
+    top, bot = pl.ds(0, half), pl.ds(half, half)
+    vocab, width = w_out.shape
+    n_full = vocab // ROWS
+    rest = vocab - n_full * ROWS
+    s_o, s_up, s_down = RING - 5, RING - 4, RING - 2
+
+    def dev(c, k):
+        return {'tp': 2 * c + k}
+
+    ld_res = pltpu.make_async_copy(hidden.at[:, pl.ds(pl.multiple_of(me * piece, piece), piece)], resid, small_sem.at[0])
+    ld_o = pltpu.make_async_copy(w_o, ring.at[s_o, pl.ds(0, w_o.shape[0])], w_sem.at[s_o])
+    ld_up = []
+    for i in range(width // ROWS):
+        ld_up.append(pltpu.make_async_copy(w_up.at[pl.ds(i * ROWS, ROWS)], ring.at[s_up + i // 3, :, pl.ds((i % 3) * w_up.shape[1], w_up.shape[1])], small_sem.at[4 + i]))
+    ld_down = [pltpu.make_async_copy(w_down.at[pl.ds(i * ROWS, ROWS)], ring.at[s_down + i], small_sem.at[1 + i]) for i in range(2)]
+    ld_last = pltpu.make_async_copy(w_out.at[pl.ds(n_full * ROWS, rest)], last, small_sem.at[3])
+
+    def ld_tile(tile):
+        slot = lax.rem(tile, RING)
+        return pltpu.make_async_copy(w_out.at[pl.ds(pl.multiple_of(tile * ROWS, ROWS), ROWS)], ring.at[slot], w_sem.at[slot])
+
+    ld_o.start()
+    ld_res.start()
+    for c in ld_up:
+        c.start()
+    for c in ld_down:
+        c.start()
+    for tile in range(s_o):
+        ld_tile(tile).start()
+    ld_last.start()
+
+    barrier = pltpu.get_barrier_semaphore()
+    for d in range(1, ways):
+        pl.semaphore_signal(barrier, inc=1, device_id={'tp': lax.rem(me + d, ways)}, device_id_type=MESH)
+
+    def copy(phase, idx, src, dst, to, ridx=None):
+        ridx = idx if ridx is None else ridx
+        return pltpu.make_async_remote_copy(src_ref=src, dst_ref=dst, send_sem=send_sem.at[phase, idx], recv_sem=recv_sem.at[phase, ridx],
+                                            device_id=to, device_id_type=MESH)
+
+    def arrive(phase, idx, dst):
+        copy(phase, idx, dst, dst, dev(chip, core)).wait_recv()
+
+    def all_sum(phase, product, residual, out_cols):
+        pb = parts.at[phase]
+        sent = []
+
+        def go(c):
+            c.start()
+            sent.append(c)
+
+        def term(c):
+            value = product(c).astype(BF16)
+            pb[2 * c] = value[:, :piece]
+            pb[2 * c + 1] = value[:, piece:]
+
+        g = gath.at[phase]
+        term(far)
+        if phase == 0:
+            pl.semaphore_wait(barrier, ways - 1)
+        for k in range(2):
+            go(copy(phase, k, pb.at[2 * far + k, top], raw1.at[phase, 0, core], dev(right, k), core))
+            go(copy(phase, 2 + k, pb.at[2 * far + k, bot], raw1.at[phase, 1, core], dev(left, k), 2 + core))
+        term(right)
+        for k in range(2):
+            go(copy(phase, 6 + k, pb.at[2 * right + k, bot], raw2.at[phase, 1, core], dev(right, k), 6 + core))
+        go(copy(phase, 9, pb.at[2 * right + other, top], sibh.at[phase, 0], dev(chip, other)))
+        term(left)
+        for k in range(2):
+            go(copy(phase, 4 + k, pb.at[2 * left + k, top], raw2.at[phase, 0, core], dev(left, k), 4 + core))
+        go(copy(phase, 10, pb.at[2 * left + other, bot], sibh.at[phase, 1], dev(chip, other)))
+        term(chip)
+        go(copy(phase, 8, pb.at[2 * chip + other], sib.at[phase], dev(chip, other)))
+        for side, (to, rws) in enumerate(((right, top), (left, bot))):
+            for k in range(2):
+                arrive(phase, 2 * side + k, raw1.at[phase, side, k])
+            arrive(phase, 9 + side, sibh.at[phase, side])
+            send3[phase, side] = (raw1[phase, side, 0].astype(F32) + raw1[phase, side, 1].astype(F32)
+                                  + pb[2 * to + core, rws].astype(F32) + sibh[phase, side].astype(F32))
+            go(copy(phase, 11 + side, send3.at[phase, side], recv3.at[phase, side], dev(to, core)))
+        arrive(phase, 8, sib.at[phase])
+        for side, rws in enumerate((top, bot)):
+            for k in range(2):
+                arrive(phase, 4 + 2 * side + k, raw2.at[phase, side, k])
+            base = (residual[rws].astype(F32) + pb[me, rws].astype(F32) + sib[phase, rws].astype(F32)
+                    + raw2[phase, side, 0].astype(F32) + raw2[phase, side, 1].astype(F32))
+            arrive(phase, 11 + side, recv3.at[phase, side])
+            value = (base + recv3[phase, side]).astype(BF16)
+            own[phase, rws] = value
+            g[me, rws] = value
+        ob = own.at[phase]
+        go(copy(phase, 13, ob.at[top], g.at[me, top], dev(right, core)))
+        go(copy(phase, 16, ob.at[bot], g.at[me, bot], dev(left, core)))
+        go(copy(phase, 19, ob, g.at[me], dev(chip, other)))
+        go(copy(phase, 14, ob.at[bot], g.at[me, bot], dev(right, core)))
+        go(copy(phase, 15, ob.at[top], g.at[me, top], dev(left, core)))
+        ml, mr, mf = 2 * left + core, 2 * right + core, 2 * far + core
+        arrive(phase, 13, g.at[ml, top])
+        go(copy(phase, 17, g.at[ml, top], g.at[ml, top], dev(right, core)))
+        arrive(phase, 16, g.at[mr, bot])
+        go(copy(phase, 18, g.at[mr, bot], g.at[mr, bot], dev(left, core)))
+        go(copy(phase, 20, g.at[ml, top], g.at[ml, top], dev(chip, other)))
+        go(copy(phase, 21, g.at[mr, bot], g.at[mr, bot], dev(chip, other)))
+        arrive(phase, 14, g.at[ml, bot])
+        go(copy(phase, 22, g.at[ml, bot], g.at[ml, bot], dev(chip, other)))
+        arrive(phase, 15, g.at[mr, top])
+        go(copy(phase, 23, g.at[mr, top], g.at[mr, top], dev(chip, other)))
+        arrive(phase, 17, g.at[mf, top])
+        go(copy(phase, 24, g.at[mf, top], g.at[mf, top], dev(chip, other)))
+        arrive(phase, 18, g.at[mf, bot])
+        go(copy(phase, 25, g.at[mf, bot], g.at[mf, bot], dev(chip, other)))
+        ol, orr, of = 2 * left + other, 2 * right + other, 2 * far + other
+        arrive(phase, 19, g.at[2 * chip + other])
+        arrive(phase, 20, g.at[ol, top])
+        arrive(phase, 21, g.at[orr, bot])
+        arrive(phase, 22, g.at[ol, bot])
+        arrive(phase, 23, g.at[orr, top])
+        arrive(phase, 24, g.at[of, top])
+        arrive(phase, 25, g.at[of, bot])
+        return sent
+
+    ld_o.wait()
+    ld_res.wait()
+    depth_o = w_o.shape[0]
+
+    def product_o(c):
+        return dotf(attended[...], ring[s_o, 0:depth_o, pl.ds(pl.multiple_of(2 * piece * c, 2 * piece), 2 * piece)])
+
+    sent = all_sum(0, product_o, resid, None)
+    ld_tile(s_o).start()
+    norm_chunks(gath.at[0], gain2, bias2, normed)
+
+    for c in ld_up:
+        c.wait()
+    ff = w_up.shape[1]
+    for n in range(0, ff, 256):
+        total = jnp.zeros((rows, 256), F32)
+        for i in range(width // ROWS):
+            total = total + dotf(normed[:, i * ROWS:(i + 1) * ROWS], ring[s_up + i // 3, :, (i % 3) * ff + n:(i % 3) * ff + n + 256])
+        act[:, n:n + 256] = jnp.square(jnp.maximum(total, 0.0)).astype(BF16)
+    ld_tile(s_up).start()
+    ld_tile(s_up + 1).start()
+    for c in ld_down:
+        c.wait()
+
+    def product_down(c):
+        cols = pl.ds(pl.multiple_of(2 * piece * c, 2 * piece), 2 * piece)
+        return dotf(act[:, :ROWS], ring[s_down, :, cols]) + dotf(act[:, ROWS:], ring[s_down + 1, :, cols])
+
+    sent += all_sum(1, product_down, gath.at[0, me], None)
+    ld_tile(s_down).start()
+    ld_tile(s_down + 1).start()
+    norm_chunks(gath.at[1], gainf, biasf, normed)
+    for j in range(ways):
+        y_out[:, j * piece:(j + 1) * piece] = gath[1, j]
+        normed_t[j * piece:(j + 1) * piece] = normed[:, j * piece:(j + 1) * piece].T
+
+    def reduce_tile(z, carry):
+        peak, total = carry
+        z3 = z.reshape(z.shape[0] // 8, 8, z.shape[1])
+        new_peak = jnp.maximum(peak, jnp.max(z3, axis=0))
+        total = total * jnp.exp(peak - new_peak) + jnp.sum(jnp.exp(z3 - new_peak[None]), axis=0)
+        return new_peak, total
+
+    def step(tile, carry):
+        slot = lax.rem(tile, RING)
+        ld_tile(tile).wait()
+        z = dotf(ring[slot], normed_t[...])
+        logits[pl.ds(pl.multiple_of(tile * ROWS, ROWS), ROWS)] = z
+
+        @pl.when(tile + RING < n_full)
+        def _():
+            ld_tile(tile + RING).start()
+        return reduce_tile(z, carry)
+
+    carry = (jnp.full((8, rows), -1e30, F32), jnp.zeros((8, rows), F32))
+    carry = lax.fori_loop(0, n_full, step, carry)
+    ld_last.wait()
+    z = dotf(last[...], normed_t[...])
+    logits[pl.ds(n_full * ROWS, rest)] = z
+    peak8, total8 = reduce_tile(z, carry)
+    peak = jnp.max(peak8, axis=0, keepdims=True)
+    total = jnp.sum(total8 * jnp.exp(peak8 - peak), axis=0, keepdims=True)
+    row = lax.broadcasted_iota(jnp.int32, (8, rows), 0)
+    stats[me] = jnp.where(row == 0, peak, total)
+    stat_out = []
+    for d in range(1, ways):
+        c = pltpu.make_async_remote_copy(src_ref=stats.at[me], dst_ref=stats.at[me], send_sem=stat_send.at[d], recv_sem=stat_recv.at[d],
+                                         device_id={'tp': lax.rem(me + d, ways)}, device_id_type=MESH)
+        c.start()
+        stat_out.append(c)
+    for d in range(1, ways):
+        src = lax.rem(me + ways - d, ways)
+        pltpu.make_async_remote_copy(src_ref=stats.at[src], dst_ref=stats.at[src], send_sem=stat_send.at[d], recv_sem=stat_recv.at[d],
+                                     device_id={'tp': me}, device_id_type=MESH).wait_recv()
+    all_stats = stats[...]
+    peaks = all_stats[:, 0, :]
+    totals = all_stats[:, 1, :]
+    top_peak = jnp.max(peaks, axis=0, keepdims=True)
+    whole = jnp.sum(totals * jnp.exp(peaks - top_peak), axis=0, keepdims=True)
+    norm_out[...] = jnp.broadcast_to(top_peak + jnp.log(whole), norm_out.shape)
+    for c in sent + stat_out:
+        c.wait_send()
+
+
+def run_tail(ways, attended, hidden, w_o, w_up, w_down, w_out_t, gain2, bias2, gainf, biasf):
+    rows, width = hidden.shape
     piece = width // ways
-    received = lax.all_to_all(partial, 'tp', 1, 0, tiled=True)
-    summed = jnp.sum(received.reshape(ways, batch, piece).astype(jnp.float32), axis=0)
-    start = lax.axis_index('tp') * piece
-    own_resid = lax.dynamic_slice_in_dim(residual, start, piece, axis=1)
-    own_sum = (own_resid.astype(jnp.float32) + summed).astype(jnp.bfloat16)
-    return lax.all_gather(own_sum, 'tp', axis=1, tiled=True)
+    half = rows // 2
+    vocab = w_out_t.shape[0]
+    rest = vocab % ROWS
+    ff = w_up.shape[1]
+    any_ = pl.BlockSpec(memory_space=pl.ANY)
+    vmem = pl.BlockSpec(memory_space=pltpu.VMEM)
+    hbm = pl.BlockSpec(memory_space=pltpu.HBM)
+    return pl.pallas_call(
+        functools.partial(tail_kernel, ways),
+        out_shape=(pltpu.VMEM((vocab, rows), F32), pltpu.VMEM((8, rows), F32), pltpu.VMEM((rows, width), BF16)),
+        in_specs=[vmem, hbm, hbm, hbm, hbm, hbm, vmem, vmem, vmem, vmem],
+        out_specs=(vmem, vmem, vmem),
+        scratch_shapes=[
+            pltpu.VMEM((RING, ROWS, width), BF16),
+            pltpu.VMEM((rest, width), BF16),
+            pltpu.VMEM((rows, piece), BF16),
+            pltpu.VMEM((rows, ff), BF16),
+            pltpu.VMEM((rows, width), BF16),
+            pltpu.VMEM((width, rows), BF16),
+            pltpu.VMEM((2, ways, rows, piece), BF16),
+            pltpu.VMEM((2, 2, 2, half, piece), BF16),
+            pltpu.VMEM((2, 2, 2, half, piece), BF16),
+            pltpu.VMEM((2, rows, piece), BF16),
+            pltpu.VMEM((2, 2, half, piece), BF16),
+            pltpu.VMEM((2, 2, half, piece), F32),
+            pltpu.VMEM((2, 2, half, piece), F32),
+            pltpu.VMEM((2, rows, piece), BF16),
+            pltpu.VMEM((2, ways, rows, piece), BF16),
+            pltpu.VMEM((ways, 8, rows), F32),
+            pltpu.SemaphoreType.DMA((RING,)),
+            pltpu.SemaphoreType.DMA((10,)),
+            pltpu.SemaphoreType.DMA((2, NSEM)),
+            pltpu.SemaphoreType.DMA((2, NSEM)),
+            pltpu.SemaphoreType.DMA((ways,)),
+            pltpu.SemaphoreType.DMA((ways,)),
+        ],
+        compiler_params=pltpu.CompilerParams(collective_id=0, has_side_effects=True, vmem_limit_bytes=LIMIT),
+        name='tail',
+    )(attended, hidden, w_o, w_up, w_down, w_out_t, gain2, bias2, gainf, biasf)
+
+
+LIMIT = 54 * 1024 * 1024
+
+
+def finish_kernel(logits, norm, y, out, y_out, sem):
+    copy = pltpu.make_async_copy(y, y_out, sem)
+
+    @pl.when(pl.program_id(0) == 0)
+    def _():
+        copy.start()
+
+    block = out.shape[0]
+    start = pl.multiple_of(pl.program_id(0) * block, 8)
+    out[...] = logits[pl.ds(start, block)] - norm[0:1]
+
+    @pl.when(pl.program_id(0) == pl.num_programs(0) - 1)
+    def _():
+        copy.wait()
+
+
+def run_finish(logits, norm, y):
+    vocab, rows = logits.shape
+    block = vocab // 12
+    vmem = pl.BlockSpec(memory_space=pltpu.VMEM)
+    return pl.pallas_call(
+        finish_kernel,
+        grid=(12,),
+        out_shape=(jax.ShapeDtypeStruct((vocab, rows), F32), jax.ShapeDtypeStruct(y.shape, BF16)),
+        in_specs=[vmem, vmem, vmem],
+        out_specs=(pl.BlockSpec((block, rows), lambda i: (i, 0)), pl.BlockSpec(memory_space=pltpu.HBM)),
+        scratch_shapes=[pltpu.SemaphoreType.DMA],
+        compiler_params=pltpu.CompilerParams(vmem_limit_bytes=8 * 1024 * 1024),
+        name='finish',
+    )(logits, norm, y)
 
 
 def solution(mesh):
@@ -73,21 +398,9 @@
 
     def local_step(new_hidden, cache_k, cache_v, lengths, ln1_gain, ln1_bias, w_q, w_k, w_v, w_o, ln2_gain, ln2_bias, w_up, w_down, lnf_gain, lnf_bias, w_out):
         attended, new_cache_k, new_cache_v = project_and_attend(new_hidden, cache_k, cache_v, lengths, ln1_gain, ln1_bias, w_q, w_k, w_v)
-        partial_o = jnp.dot(attended, w_o, preferred_element_type=jnp.float32).astype(jnp.bfloat16)
-        mid_hidden = reduce_to_all(partial_o, new_hidden, ways)
-        normed_mid = layer_norm1p(mid_hidden.astype(jnp.float32), ln2_gain, ln2_bias).astype(jnp.bfloat16)
-        up_proj = jnp.dot(normed_mid, w_up, preferred_element_type=jnp.float32)
-        activated = jnp.square(jnp.maximum(up_proj, 0.0)).astype(jnp.bfloat16)
-        partial_m = jnp.dot(activated, w_down, preferred_element_type=jnp.float32).astype(jnp.bfloat16)
-        out_hidden = reduce_to_all(partial_m, mid_hidden, ways)
-        normed_out = layer_norm1p(out_hidden.astype(jnp.float32), lnf_gain, lnf_bias).astype(jnp.bfloat16)
-        logits = jnp.dot(normed_out, w_out, preferred_element_type=jnp.float32)
-        local_peak = jnp.max(logits, axis=-1)
-        local_total = jnp.sum(jnp.exp(logits - local_peak[:, None]), axis=-1)
-        gathered = lax.all_gather(jnp.stack([local_peak, local_total]), 'tp')
-        global_peak = jnp.max(gathered[:, 0], axis=0)
-        global_total = jnp.sum(gathered[:, 1] * jnp.exp(gathered[:, 0] - global_peak[None, :]), axis=0)
-        log_probs = logits - (global_peak + jnp.log(global_total))[:, None]
-        return log_probs, new_cache_k, new_cache_v, out_hidden
+        logits, norm, y = run_tail(ways, attended, new_hidden, w_o, w_up, w_down, w_out.T,
+                                   ln2_gain[None], ln2_bias[None], lnf_gain[None], lnf_bias[None])
+        log_probs_t, out_hidden = run_finish(logits, norm, y)
+        return log_probs_t.T, new_cache_k, new_cache_v, out_hidden
 
     return jax.shard_map(local_step, mesh=mesh, in_specs=in_specs, out_specs=out_specs, check_vma=False)

time: 161 us -> 111 us (0.69)
  Pallas kernels: 0 us -> 87.8 us
  matrix products: 53.6 us -> 8.56 us
  blocking collectives: 38.4 us -> 0 us
  waiting for transfers between devices: 24.2 us -> 0 us
  other arithmetic: 23.5 us -> 9.66 us
  starting transfers between devices: 10.4 us -> 0 us
  local copies, waits for them, and re-layouts: 8.64 us -> 3.23 us
    pallas_call x0 -> x2, Pallas kernels: none -> 87.8 us  [the longest x1 82 us: run_tail(): pl.pallas_call(functools.partial(tail_kernel, ways), out_shape=(pltpu.VME...]
    dot_general x3 -> x0, matrix products: 46 us -> none  [the longest x1 38 us: local_step(): logits = jnp.dot(normed_out, w_out, preferred_element_type=jnp.float32)]
    all_gather x3 -> x0, blocking collectives: 38.4 us -> none  [the longest x2 29.6 us: reduce_to_all(): return lax.all_gather(own_sum, 'tp', axis=1, tiled=True)]
    all_to_all x2 -> x0, waiting for transfers between devices: 24.2 us -> none  [reduce_to_all(): received = lax.all_to_all(partial, 'tp', 1, 0, tiled=True)]
    all_to_all x2 -> x0, starting transfers between devices: 10.4 us -> none  [reduce_to_all(): received = lax.all_to_all(partial, 'tp', 1, 0, tiled=True)]
    reduce_sum x4 -> x0, other arithmetic: 4.7 us -> none  [the longest x2 2.51 us: reduce_to_all(): jnp.sum(received.reshape(ways, batch, piece).astype(jnp.float32), axis=0)]
    sub x1 -> x0, other arithmetic: 3.62 us -> none  [local_step(): log_probs = logits - (global_peak + jnp.log(global_total))[:, None]]
    all_to_all x2 -> x0, local copies, waits for them, and re-layouts: 3.08 us -> none  [reduce_to_all(): received = lax.all_to_all(partial, 'tp', 1, 0, tiled=True)]
  transfers between devices with their start and end apart: 2 -> 0, of which waited for: 2 -> 0; matrix products, arithmetic and copies ran while one was open for 0% -> 0% of each run, Pallas kernels for 0% -> 0%
where the time goes in v1:
time: 111 us; the launch traced here: 110 us
  Pallas kernels  87.8 us (79%)
  other arithmetic  9.66 us (9%)
  matrix products  8.56 us (8%)
  local copies, waits for them, and re-layouts  3.23 us (3%)
    pallas_call x1, Pallas kernels, run_tail(): pl.pallas_call(functools.partial(tail_kernel, ways), out_shape=(pltpu.VME...  82 us
    pallas_call x1, Pallas kernels, run_finish(): pl.pallas_call(finish_kernel, grid=(12,), out_shape=(jax.ShapeDtypeStruct...  5.82 us
    select_n x1, other arithmetic, project_and_attend(): new_cache_k = jnp.where(write_slot, key_new[:, None], cache_k)  4.93 us
    dot_general x1, matrix products, project_and_attend(): jnp.einsum('bgrl,blgk->bgrk', attn_prob, new_cache_v, preferred_element_t...  3.46 us
    dot_general x1, matrix products, project_and_attend(): jnp.dot(normed, w_q, preferred_element_type=jnp.float32)  2.79 us

profile of v1, /device:TPU:81, one launch (start us, length us, event | category | flops | bytes accessed | tf_op | source)
XLA Modules:
  0.0 110.2 jit_solution(7174996063405897859)
XLA Ops:
  0.6 0.0 copy-start
  0.6 0.0 copy-start.2
  0.7 0.0 copy-start.6
  0.7 0.0 copy-start.3
  0.7 0.8 convert_element_type.34
  1.5 1.3 %convert_reduce_fusion = f32[128]{0:T(128)S(1)} fusion(bf16[128,3072]{1,0:T(8,128)(2,1)} %hidden.1), kind=kLoop, calls=%fused_computation.8 | loop fusion | flops 786304 | bytes 786944 | tf_op jit(solution)/shard_map/reduce_sum | solution.py:21
  2.8 1.5 %fusion.7 = f32[128]{0:T(128)S(1)} fusion(bf16[128,3072]{1,0:T(8,128)(2,1)} %hidden.1, f32[128]{0:T(128)S(1)} %broadcast_multiply_fusion), kind=kLoop, calls=%fused_computation.11 | loop fusion | flops 1572736 | bytes 787456 | tf_op jit(solution)/shard_map/reduce_sum | solution.py:23
  4.3 0.0 copy-start.4
  4.3 0.0 copy-start.5
  4.3 0.0 copy-done.3
  4.3 0.0 copy-done
  4.4 0.0 copy-done.2
  4.4 0.0 copy-done.6
  4.4 0.5 convolution_convert_fusion
  4.9 0.1 copy-done.4
  5.0 0.1 iota_compare_fusion.1
  5.0 0.4 copy-done.5
  5.4 0.6 convolution_bitcast_fusion
  6.1 0.1 fusion.34
  6.2 0.1 copy.33
  6.4 0.3 multiply_cosine_fusion
  6.7 2.8 %fusion.37 = f32[128,384]{0,1:T(8,128)S(1)} fusion(bf16[3072,384]{1,0:T(8,128)(2,1)} %param.23, bf16[128,3072]{1,0:T(8,128)(2,1)S(1)} %copy-done.2, f32[3072]{0:T(1024)S(1)} %copy-done.6, f32[3072]{0:T(1024)S(1)} %broadcast_add_fusion, f32[128]{0:T(128)S(1)} %add_rsqrt_fusion, f32[128]{0:T(128)S(1)} %broadcast_multiply_fusion), kind=kOutput, calls=%fused_computation.51 | convolution fusion | flops 304349184 | bytes 3367936 | tf_op jit(solution)/shard_map/dot_general | solution.py:43
  9.5 0.1 copy.40
  9.6 0.1 copy.39
  9.8 0.1 copy.38
  9.9 0.1 subtract_convert_fusion
  10.0 0.1 pad_maximum_fusion
  10.1 4.9 %broadcast_select_fusion.1 = (bf16[128,64,1,128]{3,1,2,0:T(8,128)(2,1)S(1)}, bf16[128,64,1,128]{3,1,2,0:T(8,128)(2,1)}) fusion(bf16[128,64,1,128]{3,1,2,0:T(8,128)(2,1)} %param.18, pred[128,64]{1,0:T(8,128)(4,1)S(1)} %get-tuple-element.25, bf16[128,128]{1,0:T(8,128)(2,1)S(1)} %copy.33, bf16[128,64,1,128]{3,1,2,0:T(8,128)(2,1)} %param.19, ...), kind=kLoop, calls=%fused_computation.6 | loop fusion | flops 2097152 | bytes 8462336 | tf_op jit(solution)/shard_map/jit(_where)/select_n | solution.py:51
  15.0 0.0 copy-start.1
  15.0 1.3 %copy-done.1 = bf16[128,64,1,128]{3,1,2,0:T(8,128)(2,1)} copy-done((bf16[128,64,1,128]{3,1,2,0:T(8,128)(2,1)}, bf16[128,64,1,128]{3,1,2,0:T(8,128)(2,1)S(1)}, u32[]{:S(2)}) %copy-start.1) | copy-done | bytes 2097176
  16.4 1.2 %fusion.15 = f32[128,3,64]{2,1,0:T(4,128)S(1)} fusion(bf16[128,64,1,128]{3,1,2,0:T(8,128)(2,1)S(1)} %get-tuple-element.20, bf16[128,3,128]{2,0,1:T(8,128)(2,1)S(1)} %pad_maximum_fusion, pred[128,64]{1,0:T(8,128)(4,1)S(1)} %get-tuple-element.24), kind=kOutput, calls=%fused_computation.17 | convolution fusion | flops 6340608 | bytes 2301952 | tf_op jit(solution)/shard_map/bgrk,blgk->bgrl/dot_general | solution.py:56
  17.5 0.4 fusion.40
  17.9 3.5 %fusion.19 = bf16[128,3,128]{2,1,0:T(4,128)(2,1)S(1)} fusion(bf16[128,64,1,128]{3,1,2,0:T(8,128)(2,1)} %get-tuple-element.21, f32[128,3]{1,0:T(8,128)S(1)} %fusion.40, f32[128,3,64]{2,1,0:T(4,128)S(1)} %fusion.15), kind=kOutput, calls=%fused_computation.19 | convolution fusion | flops 6414783 | bytes 2295296 | tf_op jit(solution)/shard_map/bgrl,blgk->bgrk/dot_general | solution.py:60
  21.4 0.1 copy.35
  21.5 0.8 copy.36.attended
  22.3 82.0 %tail.1 = (f32[16032,128]{1,0:T(8,128)S(1)}, f32[8,128]{1,0:T(8,128)S(1)}, bf16[128,3072]{1,0:T(8,128)(2,1)S(1)}) custom-call(bf16[128,384]{1,0:T(8,128)(2,1)} %copy.36.attended, bf16[128,3072]{1,0:T(8,128)(2,1)} %hidden.1, bf16[384,3072]{1,0:T(8,128)(2,1)} %w_o.1, bf16[3072,1024]{1,0:T(8,128)(2,1)} %w_up.1, bf16[1024,3072]{1,0:T(8,128)(2,1)} %w_down.1, ...), custom_call_target="tpu_custom_call" | custom-call | tf_op jit(solution)/shard_map/tail/pallas_call | solution.py:321
  104.3 5.8 %finish.1 = (f32[16032,128]{1,0:T(8,128)}, bf16[128,3072]{1,0:T(8,128)(2,1)}) custom-call(f32[16032,128]{1,0:T(8,128)S(1)} %get-tuple-element.9.logits, f32[8,128]{1,0:T(8,128)S(1)} %get-tuple-element.10.norm, bf16[128,3072]{1,0:T(8,128)(2,1)S(1)} %get-tuple-element.11.y), custom_call_target="tpu_custom_call" | custom-call | tf_op jit(solution)/shard_map/finish/pallas_call | solution.py:378
  (8 shorter events, 0.1 us)
Async XLA Ops:
  0.6 3.7 %copy-start = (bf16[3072,128]{1,0:T(8,128)(2,1)S(1)}, bf16[3072,128]{1,0:T(8,128)(2,1)}, u32[]{:S(2)}) copy-start(bf16[3072,128]{1,0:T(8,128)(2,1)} %param.25) | copy-start | bytes 2359300
  0.6 3.7 %copy-start.2 = (bf16[128,3072]{1,0:T(8,128)(2,1)S(1)}, bf16[128,3072]{1,0:T(8,128)(2,1)}, u32[]{:S(2)}) copy-start(bf16[128,3072]{1,0:T(8,128)(2,1)} %hidden.1) | copy-start | bytes 2359300
  0.7 3.7 %copy-start.6 = (f32[3072]{0:T(1024)S(1)}, f32[3072]{0:T(1024)}, u32[]{:S(2)}) copy-start(f32[3072]{0:T(1024)} %param.22) | copy-start | bytes 36868
  0.7 3.7 %copy-start.3 = (f32[3072]{0:T(1024)S(1)}, f32[3072]{0:T(1024)}, u32[]{:S(2)}) copy-start(f32[3072]{0:T(1024)} %param.21) | copy-start | bytes 36868
  4.3 0.7 copy-start.4
  4.3 1.1 %copy-start.5 = (bf16[3072,128]{1,0:T(8,128)(2,1)S(1)}, bf16[3072,128]{1,0:T(8,128)(2,1)}, u32[]{:S(2)}) copy-start(bf16[3072,128]{1,0:T(8,128)(2,1)} %param.24) | copy-start | bytes 2359300
  15.0 1.3 %copy-start.1 = (bf16[128,64,1,128]{3,1,2,0:T(8,128)(2,1)}, bf16[128,64,1,128]{3,1,2,0:T(8,128)(2,1)S(1)}, u32[]{:S(2)}) copy-start(bf16[128,64,1,128]{3,1,2,0:T(8,128)(2,1)S(1)} %get-tuple-element.20) | copy-start | bytes 6291460

commit v2 on v1

--- a/solution.py
+++ b/solution.py
@@ -1,4 +1,5 @@
 import functools
+import math
 
 import jax
 import jax.numpy as jnp
@@ -15,50 +16,6 @@
 RING = 14
 ROWS = 512
 NSEM = 26
-
-
-def layer_norm1p(values, gain, bias):
-    mean = jnp.mean(values, axis=-1, keepdims=True)
-    centered = values - mean
-    variance = jnp.mean(jnp.square(centered), axis=-1, keepdims=True)
-    return centered * lax.rsqrt(variance + EPSILON) * (1.0 + gain) + bias
-
-
-def apply_rotary(vecs, positions):
-    rot_dim = vecs.shape[-1] // 2
-    half_rot = rot_dim // 2
-    exponent = -2.0 * jnp.arange(half_rot, dtype=jnp.float32) / rot_dim
-    inv_freq = ROPE_BASE ** exponent
-    angles = positions.astype(jnp.float32)[:, None] * inv_freq[None, :]
-    cosine = jnp.cos(angles)[:, None, :]
-    sine = jnp.sin(angles)[:, None, :]
-    first = vecs[..., :half_rot]
-    second = vecs[..., half_rot:rot_dim]
-    return jnp.concatenate([first * cosine - second * sine, second * cosine + first * sine, vecs[..., rot_dim:]], axis=-1)
-
-
-def project_and_attend(new_hidden, cache_k, cache_v, lengths, ln1_gain, ln1_bias, w_q, w_k, w_v):
-    batch, cache_len, kv_heads, head_dim = cache_k.shape
-    normed = layer_norm1p(new_hidden.astype(jnp.float32), ln1_gain, ln1_bias).astype(jnp.bfloat16)
-    query = jnp.dot(normed, w_q, preferred_element_type=jnp.float32).reshape(batch, -1, head_dim)
-    key_new = jnp.dot(normed, w_k, preferred_element_type=jnp.float32).reshape(batch, kv_heads, head_dim)
-    val_new = jnp.dot(normed, w_v, preferred_element_type=jnp.float32).reshape(batch, kv_heads, head_dim)
-    query = apply_rotary(query, lengths).astype(jnp.bfloat16)
-    key_new = apply_rotary(key_new, lengths).astype(jnp.bfloat16)
-    val_new = val_new.astype(jnp.bfloat16)
-    positions = jnp.arange(cache_len)
-    write_slot = (positions[None, :] == lengths[:, None])[:, :, None, None]
-    new_cache_k = jnp.where(write_slot, key_new[:, None], cache_k)
-    new_cache_v = jnp.where(write_slot, val_new[:, None], cache_v)
-    group = query.shape[1] // kv_heads
-    q_groups = query.reshape(batch, kv_heads, group, head_dim)
-    score_scale = head_dim ** -0.5
-    scores = jnp.einsum('bgrk,blgk->bgrl', q_groups, new_cache_k, preferred_element_type=jnp.float32) * score_scale
-    valid = (positions[None, :] <= lengths[:, None])[:, None, None, :]
-    scores = jnp.where(valid, scores, -1e30)
-    attn_prob = jax.nn.softmax(scores, axis=-1).astype(jnp.bfloat16)
-    mixed = jnp.einsum('bgrl,blgk->bgrk', attn_prob, new_cache_v, preferred_element_type=jnp.float32)
-    return mixed.astype(jnp.bfloat16).reshape(batch, -1), new_cache_k, new_cache_v
 
 
 def dotf(lhs, rhs):
@@ -349,40 +306,193 @@
         ],
         compiler_params=pltpu.CompilerParams(collective_id=0, has_side_effects=True, vmem_limit_bytes=LIMIT),
         name='tail',
-    )(attended, hidden, w_o, w_up, w_down, w_out_t, gain2, bias2, gainf, biasf)
-
-
-LIMIT = 54 * 1024 * 1024
-
-
-def finish_kernel(logits, norm, y, out, y_out, sem):
-    copy = pltpu.make_async_copy(y, y_out, sem)
-
-    @pl.when(pl.program_id(0) == 0)
-    def _():
-        copy.start()
-
-    block = out.shape[0]
-    start = pl.multiple_of(pl.program_id(0) * block, 8)
-    out[...] = logits[pl.ds(start, block)] - norm[0:1]
-
-    @pl.when(pl.program_id(0) == pl.num_programs(0) - 1)
-    def _():
-        copy.wait()
+    )(pltpu.with_memory_space_constraint(attended, pltpu.VMEM), hidden, w_o, w_up, w_down, w_out_t, gain2, bias2, gainf, biasf)
+
+
+LIMIT = 53 * 1024 * 1024
+
+
+CHUNKS = 4
+
+
+def attend_kernel(hidden, lengths, gain, bias, w_q, w_k, w_v, cache_k, cache_v,
+                  attended, out_k, out_v,
+                  x, gb, len_row, normed, w_qkv, qkv, len_col, k_buf, v_buf, misc_sem, w_sem, in_sem, out_sem):
+    rows, width = hidden.shape
+    seqs, slots, dim = cache_k.shape
+    q_cols = w_q.shape[1]
+    heads = q_cols // dim
+    step_w = width // CHUNKS
+    step_s = seqs // CHUNKS
+
+    small = [pltpu.make_async_copy(hidden, x, misc_sem.at[0]),
+             pltpu.make_async_copy(gain, gb.at[pl.ds(0, 1)], misc_sem.at[1]),
+             pltpu.make_async_copy(bias, gb.at[pl.ds(1, 1)], misc_sem.at[2]),
+             pltpu.make_async_copy(lengths, len_row, misc_sem.at[3])]
+    for c in small:
+        c.start()
+    w_in = []
+    for i in range(CHUNKS):
+        part = pl.ds(i * step_w, step_w)
+        w_in.append([pltpu.make_async_copy(w_q.at[part], w_qkv.at[part, pl.ds(0, q_cols)], w_sem.at[0, i]),
+                     pltpu.make_async_copy(w_k.at[part], w_qkv.at[part, pl.ds(q_cols, dim)], w_sem.at[1, i]),
+                     pltpu.make_async_copy(w_v.at[part], w_qkv.at[part, pl.ds(q_cols + dim, dim)], w_sem.at[2, i])])
+        for c in w_in[-1]:
+            c.start()
+    kv_in, kv_out = [], []
+    for i in range(CHUNKS):
+        part = pl.ds(i * step_s, step_s)
+        kv_in.append([pltpu.make_async_copy(cache_k.at[part], k_buf.at[part], in_sem.at[0, i]),
+                      pltpu.make_async_copy(cache_v.at[part], v_buf.at[part], in_sem.at[1, i])])
+        kv_out.append([pltpu.make_async_copy(k_buf.at[part], out_k.at[part], out_sem.at[0, i]),
+                       pltpu.make_async_copy(v_buf.at[part], out_v.at[part], out_sem.at[1, i])])
+        for c in kv_in[-1]:
+            c.start()
+
+    small[3].wait()
+    lens = jnp.broadcast_to(len_row[...].astype(F32), (rows, rows)).T
+    len_col[...] = lens
+    lane = lax.broadcasted_iota(jnp.int32, (1, dim), 1)
+    half_rot = dim // 4
+    freq_lane = jnp.where(lane < half_rot, lane, lane - half_rot).astype(F32)
+    inv_freq = jnp.where(lane < 2 * half_rot, jnp.exp(freq_lane * (-2.0 / (2 * half_rot) * math.log(ROPE_BASE))), 0.0)
+    angle = lens * inv_freq
+    cosine = jnp.cos(angle)
+    sine = jnp.where(lane < half_rot, -1.0, 1.0) * jnp.sin(angle)
+    for c in small[:3]:
+        c.wait()
+    total = jnp.zeros((rows, 128), F32)
+    piece = width // 8
+    for j in range(8):
+        total = total + fold(x[:, j * piece:(j + 1) * piece].astype(F32))
+    mean = jnp.sum(total, axis=-1, keepdims=True) / width
+    total = jnp.zeros((rows, 128), F32)
+    for j in range(8):
+        total = total + fold(jnp.square(x[:, j * piece:(j + 1) * piece].astype(F32) - mean))
+    scale = lax.rsqrt(jnp.sum(total, axis=-1, keepdims=True) / width + EPSILON)
+    for j in range(8):
+        cols = slice(j * piece, (j + 1) * piece)
+        normed[:, cols] = ((x[:, cols].astype(F32) - mean) * scale * (1.0 + gb[0:1, cols]) + gb[1:2, cols]).astype(BF16)
+
+    for i in range(CHUNKS):
+        for c in w_in[i]:
+            c.wait()
+        part = slice(i * step_w, (i + 1) * step_w)
+        product = dotf(normed[:, part], w_qkv[part])
+        if i == 0:
+            qkv[...] = product
+        else:
+            qkv[...] += product
+    for h in range(heads + 1):
+        cols = slice(h * dim, (h + 1) * dim)
+        vec = qkv[:, cols]
+        partner = jnp.where(lane < half_rot, pltpu.roll(vec, dim - half_rot, 1), pltpu.roll(vec, half_rot, 1))
+        qkv[:, cols] = vec * cosine + partner * sine
+
+    row_id = lax.broadcasted_iota(jnp.int32, (slots, dim), 0).astype(F32)
+    group = 8
+    span = group * slots
+    offset = (lax.broadcasted_iota(jnp.int32, (group, span), 1) - slots * lax.broadcasted_iota(jnp.int32, (group, span), 0)).astype(F32)
+    k_cols, v_cols = slice(q_cols, q_cols + dim), slice(q_cols + dim, q_cols + 2 * dim)
+    for i in range(CHUNKS):
+        for c in kv_in[i]:
+            c.wait()
+
+        def put(s, carry):
+            base = pl.multiple_of(i * step_s + s * 8, 8)
+            lens8 = len_col[pl.ds(base, 8), :]
+            new_k = qkv[pl.ds(base, 8), k_cols]
+            new_v = qkv[pl.ds(base, 8), v_cols]
+            for t in range(8):
+                here = row_id == lens8[t:t + 1]
+                k_buf[base + t] = jnp.where(here, new_k[t:t + 1], k_buf[base + t].astype(F32)).astype(BF16)
+                v_buf[base + t] = jnp.where(here, new_v[t:t + 1], v_buf[base + t].astype(F32)).astype(BF16)
+            return carry
+
+        lax.fori_loop(0, step_s // 8, put, 0)
+        for c in kv_out[i]:
+            c.start()
+        for g in range(step_s // group):
+            b = i * step_s + g * group
+            q = jnp.concatenate([qkv[b:b + group, h * dim:(h + 1) * dim] for h in range(heads)], axis=0).astype(BF16)
+            keys = k_buf[b:b + group].reshape(span, dim)
+            vals = v_buf[b:b + group].reshape(span, dim)
+            scores = lax.dot_general(q, keys, (((1,), (1,)), ((), ())), preferred_element_type=F32) * (dim ** -0.5)
+            lens8 = len_col[b:b + group, 0:1]
+            valid = (offset >= 0.0) & (offset <= lens8)
+            scores = jnp.where(valid[None], scores.reshape(heads, group, span), -1e30)
+            peak = jnp.max(scores, axis=-1, keepdims=True)
+            weight = jnp.where(valid[None], jnp.exp(scores - peak), 0.0)
+            prob = (weight / jnp.sum(weight, axis=-1, keepdims=True)).astype(BF16)
+            mixed = dotf(prob.reshape(heads * group, span), vals).astype(BF16)
+            for h in range(heads):
+                attended[b:b + group, h * dim:(h + 1) * dim] = mixed[h * group:(h + 1) * group]
+    for pair in kv_out:
+        for c in pair:
+            c.wait()
+
+
+def run_attend(hidden, cache_k, cache_v, lengths, gain, bias, w_q, w_k, w_v):
+    rows, width = hidden.shape
+    seqs, slots, dim = cache_k.shape
+    q_cols = w_q.shape[1]
+    hbm = pl.BlockSpec(memory_space=pltpu.HBM)
+    vmem = pl.BlockSpec(memory_space=pltpu.VMEM)
+    return pl.pallas_call(
+        attend_kernel,
+        out_shape=(pltpu.VMEM((rows, q_cols), BF16), jax.ShapeDtypeStruct(cache_k.shape, BF16), jax.ShapeDtypeStruct(cache_v.shape, BF16)),
+        in_specs=[hbm] * 9,
+        out_specs=(vmem, hbm, hbm),
+        scratch_shapes=[
+            pltpu.VMEM((rows, width), BF16),
+            pltpu.VMEM((8, width), F32),
+            pltpu.VMEM((1, rows), jnp.int32),
+            pltpu.VMEM((rows, width), BF16),
+            pltpu.VMEM((width, q_cols + 2 * dim), BF16),
+            pltpu.VMEM((rows, q_cols + 2 * dim), F32),
+            pltpu.VMEM((rows, rows), F32),
+            pltpu.VMEM((seqs, slots, dim), BF16),
+            pltpu.VMEM((seqs, slots, dim), BF16),
+            pltpu.SemaphoreType.DMA((4,)),
+            pltpu.SemaphoreType.DMA((3, CHUNKS)),
+            pltpu.SemaphoreType.DMA((2, CHUNKS)),
+            pltpu.SemaphoreType.DMA((2, CHUNKS)),
+        ],
+        compiler_params=pltpu.CompilerParams(vmem_limit_bytes=62 * 1024 * 1024),
+        name='attend',
+    )(hidden, lengths, gain, bias, w_q, w_k, w_v, cache_k, cache_v)
+
+
+PARTS = 8
+
+
+def finish_kernel(logits, norm, y, out, y_out, buf, sem, y_sem):
+    copy = pltpu.make_async_copy(y, y_out, y_sem)
+    copy.start()
+    block = logits.shape[0] // PARTS // 8 * 8
+    outs = []
+    for i in range(PARTS):
+        size = block if i < PARTS - 1 else logits.shape[0] - block * (PARTS - 1)
+        part = pl.ds(i * block, size)
+        buf[part] = logits[part] - norm[0:1]
+        outs.append(pltpu.make_async_copy(buf.at[part], out.at[part], sem.at[i]))
+        outs[-1].start()
+    for c in outs:
+        c.wait()
+    copy.wait()
 
 
 def run_finish(logits, norm, y):
     vocab, rows = logits.shape
-    block = vocab // 12
     vmem = pl.BlockSpec(memory_space=pltpu.VMEM)
+    hbm = pl.BlockSpec(memory_space=pltpu.HBM)
     return pl.pallas_call(
         finish_kernel,
-        grid=(12,),
         out_shape=(jax.ShapeDtypeStruct((vocab, rows), F32), jax.ShapeDtypeStruct(y.shape, BF16)),
         in_specs=[vmem, vmem, vmem],
-        out_specs=(pl.BlockSpec((block, rows), lambda i: (i, 0)), pl.BlockSpec(memory_space=pltpu.HBM)),
-        scratch_shapes=[pltpu.SemaphoreType.DMA],
-        compiler_params=pltpu.CompilerParams(vmem_limit_bytes=8 * 1024 * 1024),
+        out_specs=(hbm, hbm),
+        scratch_shapes=[pltpu.VMEM((vocab, rows), F32), pltpu.SemaphoreType.DMA((PARTS,)), pltpu.SemaphoreType.DMA],
+        compiler_params=pltpu.CompilerParams(vmem_limit_bytes=16 * 1024 * 1024),
         name='finish',
     )(logits, norm, y)
 
@@ -397,10 +507,12 @@
     out_specs = (P('bs', 'tp'), cache_spec, cache_spec, row_spec)
 
     def local_step(new_hidden, cache_k, cache_v, lengths, ln1_gain, ln1_bias, w_q, w_k, w_v, w_o, ln2_gain, ln2_bias, w_up, w_down, lnf_gain, lnf_bias, w_out):
-        attended, new_cache_k, new_cache_v = project_and_attend(new_hidden, cache_k, cache_v, lengths, ln1_gain, ln1_bias, w_q, w_k, w_v)
+        shape = cache_k.shape
+        flat = (shape[0], shape[1], shape[3])
+        attended, new_cache_k, new_cache_v = run_attend(new_hidden, cache_k.reshape(flat), cache_v.reshape(flat), lengths[None], ln1_gain[None], ln1_bias[None], w_q, w_k, w_v)
         logits, norm, y = run_tail(ways, attended, new_hidden, w_o, w_up, w_down, w_out.T,
                                    ln2_gain[None], ln2_bias[None], lnf_gain[None], lnf_bias[None])
         log_probs_t, out_hidden = run_finish(logits, norm, y)
-        return log_probs_t.T, new_cache_k, new_cache_v, out_hidden
+        return log_probs_t.T, new_cache_k.reshape(shape), new_cache_v.reshape(shape), out_hidden
 
     return jax.shard_map(local_step, mesh=mesh, in_specs=in_specs, out_specs=out_specs, check_vma=False)

time: 111 us -> 98.5 us (0.89)
  Pallas kernels: 87.8 us -> 97.7 us
  other arithmetic: 9.66 us -> 0 us
  matrix products: 8.56 us -> 0 us
  local copies, waits for them, and re-layouts: 3.23 us -> 0 us
    pallas_call x1 -> x2, Pallas kernels: 5.82 us -> 16.1 us  [the longest x1 12.5 us: run_attend(): pl.pallas_call(attend_kernel, out_shape=(pltpu.VMEM((rows, q_cols), BF16)...]
    dot_general x5 -> x0, matrix products: 8.56 us -> none  [the longest x1 3.46 us: project_and_attend(): jnp.einsum('bgrl,blgk->bgrk', attn_prob, new_cache_v, preferred_element_t...]
    select_n x1 -> x0, other arithmetic: 4.93 us -> none  [project_and_attend(): new_cache_k = jnp.where(write_slot, key_new[:, None], cache_k)]
    reduce_sum x2 -> x0, other arithmetic: 2.82 us -> none  [the longest x1 1.49 us: layer_norm1p(): variance = jnp.mean(jnp.square(centered), axis=-1, keepdims=True)]
    unnamed x17 -> x0, local copies, waits for them, and re-layouts: 2.2 us -> none
where the time goes in v2:
time: 98.5 us; the launch traced here: 98.3 us
  Pallas kernels  97.7 us (99%)
    pallas_call x1, Pallas kernels, run_tail(): pl.pallas_call(functools.partial(tail_kernel, ways), out_shape=(pltpu.VME...  81.6 us
    pallas_call x1, Pallas kernels, run_attend(): pl.pallas_call(attend_kernel, out_shape=(pltpu.VMEM((rows, q_cols), BF16)...  12.5 us
    pallas_call x1, Pallas kernels, run_finish(): pl.pallas_call(finish_kernel, out_shape=(jax.ShapeDtypeStruct((vocab, row...  3.58 us

profile of v2, /device:TPU:81, one launch (start us, length us, event | category | flops | bytes accessed | tf_op | source)
XLA Modules:
  0.0 98.3 jit_solution(12231711953067701374)
XLA Ops:
  0.6 12.5 %attend.1 = (bf16[128,384]{1,0:T(8,128)(2,1)S(1)}, bf16[128,64,128]{2,1,0:T(8,128)(2,1)}, bf16[128,64,128]{2,1,0:T(8,128)(2,1)}) custom-call(bf16[128,3072]{1,0:T(8,128)(2,1)} %hidden.3, s32[1,128]{1,0:T(1,128)} %bitcast.25, f32[1,3072]{1,0:T(1,128)} %bitcast.23, f32[1,3072]{1,0:T(1,128)} %bitcast.24, bf16[3072,384]{1,0:T(8,128)(2,1)} %w_q.1, ...), custom_call_target="tpu_custom_call" | custom-call | tf_op jit(solution)/shard_map/attend/pallas_call | solution.py:441
  13.1 81.6 %tail.1 = (f32[16032,128]{1,0:T(8,128)S(1)}, f32[8,128]{1,0:T(8,128)S(1)}, bf16[128,3072]{1,0:T(8,128)(2,1)S(1)}) custom-call(bf16[128,384]{1,0:T(8,128)(2,1)S(1)} %get-tuple-element.12.attended, bf16[128,3072]{1,0:T(8,128)(2,1)} %hidden.3, bf16[384,3072]{1,0:T(8,128)(2,1)} %w_o.1, bf16[3072,1024]{1,0:T(8,128)(2,1)} %w_up.1, bf16[1024,3072]{1,0:T(8,128)(2,1)} %w_down.1, ...), custom_call_target="tpu_custom_call" | custom-call | tf_op jit(solution)/shard_map/tail/pallas_call | solution.py:278
  94.7 3.6 %finish.1 = (f32[16032,128]{1,0:T(8,128)}, bf16[128,3072]{1,0:T(8,128)(2,1)}) custom-call(f32[16032,128]{1,0:T(8,128)S(1)} %get-tuple-element.13.logits, f32[8,128]{1,0:T(8,128)S(1)} %get-tuple-element.14.norm, bf16[128,3072]{1,0:T(8,128)(2,1)S(1)} %get-tuple-element.15.y), custom_call_target="tpu_custom_call" | custom-call | tf_op jit(solution)/shard_map/finish/pallas_call | solution.py:489

commit v3 on v2

--- a/solution.py
+++ b/solution.py
@@ -14,6 +14,8 @@
 F32 = jnp.float32
 MESH = pl.DeviceIdType.MESH
 RING = 14
+FLIPS = 12
+BLOCK = 256
 ROWS = 512
 NSEM = 26
 
@@ -83,13 +85,27 @@
 
     ld_o.start()
     ld_res.start()
+    for tile in range(4):
+        ld_tile(tile).start()
     for c in ld_up:
         c.start()
     for c in ld_down:
         c.start()
-    for tile in range(s_o):
+    for tile in range(4, s_o):
         ld_tile(tile).start()
     ld_last.start()
+
+    def flip(tile):
+        ld_tile(tile).wait()
+
+        def turn(b, carry):
+            for part in range(2):
+                cols = pl.ds(pl.multiple_of((2 * b + part) * BLOCK, BLOCK), BLOCK)
+                for a in range(0, ROWS, BLOCK):
+                    ring[tile, a:a + BLOCK, cols] = ring[tile, a:a + BLOCK, cols].T
+            return carry
+
+        lax.fori_loop(0, width // BLOCK // 2, turn, 0)
 
     barrier = pltpu.get_barrier_semaphore()
     for d in range(1, ways):
@@ -103,7 +119,7 @@
     def arrive(phase, idx, dst):
         copy(phase, idx, dst, dst, dev(chip, core)).wait_recv()
 
-    def all_sum(phase, product, residual, out_cols):
+    def all_sum(phase, product, residual, fill):
         pb = parts.at[phase]
         sent = []
 
@@ -133,6 +149,8 @@
         go(copy(phase, 10, pb.at[2 * left + other, bot], sibh.at[phase, 1], dev(chip, other)))
         term(chip)
         go(copy(phase, 8, pb.at[2 * chip + other], sib.at[phase], dev(chip, other)))
+        for tile in fill[0]:
+            flip(tile)
         for side, (to, rws) in enumerate(((right, top), (left, bot))):
             for k in range(2):
                 arrive(phase, 2 * side + k, raw1.at[phase, side, k])
@@ -140,6 +158,8 @@
             send3[phase, side] = (raw1[phase, side, 0].astype(F32) + raw1[phase, side, 1].astype(F32)
                                   + pb[2 * to + core, rws].astype(F32) + sibh[phase, side].astype(F32))
             go(copy(phase, 11 + side, send3.at[phase, side], recv3.at[phase, side], dev(to, core)))
+        for tile in fill[1]:
+            flip(tile)
         arrive(phase, 8, sib.at[phase])
         for side, rws in enumerate((top, bot)):
             for k in range(2):
@@ -156,6 +176,8 @@
         go(copy(phase, 19, ob, g.at[me], dev(chip, other)))
         go(copy(phase, 14, ob.at[bot], g.at[me, bot], dev(right, core)))
         go(copy(phase, 15, ob.at[top], g.at[me, top], dev(left, core)))
+        for tile in fill[2]:
+            flip(tile)
         ml, mr, mf = 2 * left + core, 2 * right + core, 2 * far + core
         arrive(phase, 13, g.at[ml, top])
         go(copy(phase, 17, g.at[ml, top], g.at[ml, top], dev(right, core)))
@@ -163,6 +185,8 @@
         go(copy(phase, 18, g.at[mr, bot], g.at[mr, bot], dev(left, core)))
         go(copy(phase, 20, g.at[ml, top], g.at[ml, top], dev(chip, other)))
         go(copy(phase, 21, g.at[mr, bot], g.at[mr, bot], dev(chip, other)))
+        for tile in fill[3]:
+            flip(tile)
         arrive(phase, 14, g.at[ml, bot])
         go(copy(phase, 22, g.at[ml, bot], g.at[ml, bot], dev(chip, other)))
         arrive(phase, 15, g.at[mr, top])
@@ -188,7 +212,7 @@
     def product_o(c):
         return dotf(attended[...], ring[s_o, 0:depth_o, pl.ds(pl.multiple_of(2 * piece * c, 2 * piece), 2 * piece)])
 
-    sent = all_sum(0, product_o, resid, None)
+    sent = all_sum(0, product_o, resid, ((0,), (1, 2), (3,), (4,)))
     ld_tile(s_o).start()
     norm_chunks(gath.at[0], gain2, bias2, normed)
 
@@ -209,7 +233,7 @@
         cols = pl.ds(pl.multiple_of(2 * piece * c, 2 * piece), 2 * piece)
         return dotf(act[:, :ROWS], ring[s_down, :, cols]) + dotf(act[:, ROWS:], ring[s_down + 1, :, cols])
 
-    sent += all_sum(1, product_down, gath.at[0, me], None)
+    sent += all_sum(1, product_down, gath.at[0, me], ((5,), (6, 7, 8), (9, 10), (11,)))
     ld_tile(s_down).start()
     ld_tile(s_down + 1).start()
     norm_chunks(gath.at[1], gainf, biasf, normed)
@@ -224,20 +248,45 @@
         total = total * jnp.exp(peak - new_peak) + jnp.sum(jnp.exp(z3 - new_peak[None]), axis=0)
         return new_peak, total
 
+    def rows_of(tile):
+        return pl.ds(pl.multiple_of(tile * ROWS, ROWS), ROWS)
+
+    def refill(tile):
+        @pl.when(tile + RING < n_full)
+        def _():
+            ld_tile(tile + RING).start()
+
+    def step_turned(pair, carry):
+        for t in range(2):
+            before = jnp.maximum(2 * pair - 2 + t, 0)
+            carry = reduce_tile(logits[rows_of(before)], carry)
+        for t in range(2):
+            tile = 2 * pair + t
+            for a in range(0, ROWS, BLOCK):
+                z = jnp.zeros((rows, BLOCK), F32)
+                for b in range(0, width, BLOCK):
+                    z = z + dotf(normed[:, b:b + BLOCK], ring[tile, a:a + BLOCK, b:b + BLOCK])
+                logits[pl.ds(pl.multiple_of(tile * ROWS + a, BLOCK), BLOCK)] = z.T
+        for t in range(2):
+            refill(2 * pair + t)
+        return carry
+
     def step(tile, carry):
         slot = lax.rem(tile, RING)
         ld_tile(tile).wait()
-        z = dotf(ring[slot], normed_t[...])
-        logits[pl.ds(pl.multiple_of(tile * ROWS, ROWS), ROWS)] = z
-
-        @pl.when(tile + RING < n_full)
-        def _():
-            ld_tile(tile + RING).start()
-        return reduce_tile(z, carry)
-
+        carry = reduce_tile(logits[rows_of(tile - 1)], carry)
+        logits[rows_of(tile)] = dotf(ring[slot], normed_t[...])
+        refill(tile)
+        return carry
+
+    logits[pl.ds(0, 2 * ROWS)] = jnp.full((2 * ROWS, rows), -1e30, F32)
     carry = (jnp.full((8, rows), -1e30, F32), jnp.zeros((8, rows), F32))
-    carry = lax.fori_loop(0, n_full, step, carry)
+    carry = lax.fori_loop(0, FLIPS // 2, step_turned, carry)
+    last_turned = FLIPS // 2 * 2
+    carry = reduce_tile(logits[rows_of(last_turned - 2)], carry)
+    carry = lax.fori_loop(last_turned, n_full, step, carry)
     ld_last.wait()
+    carry = reduce_tile(logits[rows_of(n_full - 1)], carry)
     z = dotf(last[...], normed_t[...])
     logits[pl.ds(n_full * ROWS, rest)] = z
     peak8, total8 = reduce_tile(z, carry)
@@ -313,6 +362,7 @@
 
 
 CHUNKS = 4
+PROJ = 2
 
 
 def attend_kernel(hidden, lengths, gain, bias, w_q, w_k, w_v, cache_k, cache_v,
@@ -322,7 +372,7 @@
     seqs, slots, dim = cache_k.shape
     q_cols = w_q.shape[1]
     heads = q_cols // dim
-    step_w = width // CHUNKS
+    step_w = width // PROJ
     step_s = seqs // CHUNKS
 
     small = [pltpu.make_async_copy(hidden, x, misc_sem.at[0]),
@@ -332,7 +382,7 @@
     for c in small:
         c.start()
     w_in = []
-    for i in range(CHUNKS):
+    for i in range(PROJ):
         part = pl.ds(i * step_w, step_w)
         w_in.append([pltpu.make_async_copy(w_q.at[part], w_qkv.at[part, pl.ds(0, q_cols)], w_sem.at[0, i]),
                      pltpu.make_async_copy(w_k.at[part], w_qkv.at[part, pl.ds(q_cols, dim)], w_sem.at[1, i]),
@@ -374,7 +424,7 @@
         cols = slice(j * piece, (j + 1) * piece)
         normed[:, cols] = ((x[:, cols].astype(F32) - mean) * scale * (1.0 + gb[0:1, cols]) + gb[1:2, cols]).astype(BF16)
 
-    for i in range(CHUNKS):
+    for i in range(PROJ):
         for c in w_in[i]:
             c.wait()
         part = slice(i * step_w, (i + 1) * step_w)
@@ -412,19 +462,22 @@
         lax.fori_loop(0, step_s // 8, put, 0)
         for c in kv_out[i]:
             c.start()
-        for g in range(step_s // group):
-            b = i * step_s + g * group
+        groups = [i * step_s + g * group for g in range(step_s // group)]
+        all_scores = []
+        for b in groups:
             q = jnp.concatenate([qkv[b:b + group, h * dim:(h + 1) * dim] for h in range(heads)], axis=0).astype(BF16)
             keys = k_buf[b:b + group].reshape(span, dim)
-            vals = v_buf[b:b + group].reshape(span, dim)
-            scores = lax.dot_general(q, keys, (((1,), (1,)), ((), ())), preferred_element_type=F32) * (dim ** -0.5)
-            lens8 = len_col[b:b + group, 0:1]
-            valid = (offset >= 0.0) & (offset <= lens8)
-            scores = jnp.where(valid[None], scores.reshape(heads, group, span), -1e30)
+            all_scores.append(lax.dot_general(q, keys, (((1,), (1,)), ((), ())), preferred_element_type=F32))
+        probs = []
+        for b, scores in zip(groups, all_scores):
+            valid = (offset >= 0.0) & (offset <= len_col[b:b + group, 0:1])
+            scores = jnp.where(valid[None], scores.reshape(heads, group, span) * (dim ** -0.5), -1e30)
             peak = jnp.max(scores, axis=-1, keepdims=True)
             weight = jnp.where(valid[None], jnp.exp(scores - peak), 0.0)
             prob = (weight / jnp.sum(weight, axis=-1, keepdims=True)).astype(BF16)
-            mixed = dotf(prob.reshape(heads * group, span), vals).astype(BF16)
+            probs.append(prob.reshape(heads * group, span))
+        for b, prob in zip(groups, probs):
+            mixed = dotf(prob, v_buf[b:b + group].reshape(span, dim)).astype(BF16)
             for h in range(heads):
                 attended[b:b + group, h * dim:(h + 1) * dim] = mixed[h * group:(h + 1) * group]
     for pair in kv_out:
@@ -454,7 +507,7 @@
             pltpu.VMEM((seqs, slots, dim), BF16),
             pltpu.VMEM((seqs, slots, dim), BF16),
             pltpu.SemaphoreType.DMA((4,)),
-            pltpu.SemaphoreType.DMA((3, CHUNKS)),
+            pltpu.SemaphoreType.DMA((3, PROJ)),
             pltpu.SemaphoreType.DMA((2, CHUNKS)),
             pltpu.SemaphoreType.DMA((2, CHUNKS)),
         ],

time: 98.5 us -> 90.4 us (0.918)
  Pallas kernels: 97.7 us -> 89.6 us
    pallas_call x1, Pallas kernels: 81.6 us -> 77.1 us  [run_tail(): pl.pallas_call(functools.partial(tail_kernel, ways), out_shape=(pltpu.VME...]
    pallas_call x1, Pallas kernels: 12.5 us -> 8.87 us  [run_attend(): pl.pallas_call(attend_kernel, out_shape=(pltpu.VMEM((rows, q_cols), BF16)...]
where the time goes in v3:
time: 90.4 us; the launch traced here: 90.2 us
  Pallas kernels  89.6 us (99%)
    pallas_call x1, Pallas kernels, run_tail(): pl.pallas_call(functools.partial(tail_kernel, ways), out_shape=(pltpu.VME...  77.1 us
    pallas_call x1, Pallas kernels, run_attend(): pl.pallas_call(attend_kernel, out_shape=(pltpu.VMEM((rows, q_cols), BF16)...  8.87 us
    pallas_call x1, Pallas kernels, run_finish(): pl.pallas_call(finish_kernel, out_shape=(jax.ShapeDtypeStruct((vocab, row...  3.58 us

profile of v3, /device:TPU:81, one launch (start us, length us, event | category | flops | bytes accessed | tf_op | source)
XLA Modules:
  0.0 90.2 jit_solution(2869831844515460560)
XLA Ops:
  0.6 8.9 %attend.1 = (bf16[128,384]{1,0:T(8,128)(2,1)S(1)}, bf16[128,64,128]{2,1,0:T(8,128)(2,1)}, bf16[128,64,128]{2,1,0:T(8,128)(2,1)}) custom-call(bf16[128,3072]{1,0:T(8,128)(2,1)} %hidden.3, s32[1,128]{1,0:T(1,128)} %bitcast.25, f32[1,3072]{1,0:T(1,128)} %bitcast.23, f32[1,3072]{1,0:T(1,128)} %bitcast.24, bf16[3072,384]{1,0:T(8,128)(2,1)} %w_q.1, ...), custom_call_target="tpu_custom_call" | custom-call | tf_op jit(solution)/shard_map/attend/pallas_call | solution.py:494
  9.5 77.1 %tail.1 = (f32[16032,128]{1,0:T(8,128)S(1)}, f32[8,128]{1,0:T(8,128)S(1)}, bf16[128,3072]{1,0:T(8,128)(2,1)S(1)}) custom-call(bf16[128,384]{1,0:T(8,128)(2,1)S(1)} %get-tuple-element.12.attended, bf16[128,3072]{1,0:T(8,128)(2,1)} %hidden.3, bf16[384,3072]{1,0:T(8,128)(2,1)} %w_o.1, bf16[3072,1024]{1,0:T(8,128)(2,1)} %w_up.1, bf16[1024,3072]{1,0:T(8,128)(2,1)} %w_down.1, ...), custom_call_target="tpu_custom_call" | custom-call | tf_op jit(solution)/shard_map/tail/pallas_call | solution.py:327
  86.6 3.6 %finish.1 = (f32[16032,128]{1,0:T(8,128)}, bf16[128,3072]{1,0:T(8,128)(2,1)}) custom-call(f32[16032,128]{1,0:T(8,128)S(1)} %get-tuple-element.13.logits, f32[8,128]{1,0:T(8,128)S(1)} %get-tuple-element.14.norm, bf16[128,3072]{1,0:T(8,128)(2,1)S(1)} %get-tuple-element.15.y), custom_call_target="tpu_custom_call" | custom-call | tf_op jit(solution)/shard_map/finish/pallas_call | solution.py:542

commit v4 on v3

--- a/solution.py
+++ b/solution.py
@@ -13,7 +13,7 @@
 BF16 = jnp.bfloat16
 F32 = jnp.float32
 MESH = pl.DeviceIdType.MESH
-RING = 14
+RING = 13
 FLIPS = 12
 BLOCK = 256
 ROWS = 512
@@ -50,7 +50,7 @@
 
 def tail_kernel(ways, attended, hidden, w_o, w_up, w_down, w_out, gain2, bias2, gainf, biasf,
                 logits, norm_out, y_out,
-                ring, last, resid, act, normed, normed_t, parts, raw1, raw2, sib, sibh, send3, recv3, own, gath, stats,
+                ring, turned, last, resid, act, normed, normed_t, parts, raw1, raw2, sib, sibh, send3, recv3, own, gath, stats,
                 w_sem, small_sem, send_sem, recv_sem, stat_send, stat_recv):
     me = lax.axis_index('tp')
     core = lax.rem(me, 2)
@@ -97,15 +97,18 @@
 
     def flip(tile):
         ld_tile(tile).wait()
+        target = ring.at[tile] if tile < FLIPS else turned
 
         def turn(b, carry):
             for part in range(2):
                 cols = pl.ds(pl.multiple_of((2 * b + part) * BLOCK, BLOCK), BLOCK)
                 for a in range(0, ROWS, BLOCK):
-                    ring[tile, a:a + BLOCK, cols] = ring[tile, a:a + BLOCK, cols].T
+                    target[a:a + BLOCK, cols] = ring[tile, a:a + BLOCK, cols].T
             return carry
 
         lax.fori_loop(0, width // BLOCK // 2, turn, 0)
+        if tile == FLIPS:
+            ld_tile(tile + RING).start()
 
     barrier = pltpu.get_barrier_semaphore()
     for d in range(1, ways):
@@ -119,7 +122,7 @@
     def arrive(phase, idx, dst):
         copy(phase, idx, dst, dst, dev(chip, core)).wait_recv()
 
-    def all_sum(phase, product, residual, fill):
+    def all_sum(phase, product, residual, fill, freed):
         pb = parts.at[phase]
         sent = []
 
@@ -149,6 +152,8 @@
         go(copy(phase, 10, pb.at[2 * left + other, bot], sibh.at[phase, 1], dev(chip, other)))
         term(chip)
         go(copy(phase, 8, pb.at[2 * chip + other], sib.at[phase], dev(chip, other)))
+        for tile in freed:
+            ld_tile(tile).start()
         for tile in fill[0]:
             flip(tile)
         for side, (to, rws) in enumerate(((right, top), (left, bot))):
@@ -212,8 +217,7 @@
     def product_o(c):
         return dotf(attended[...], ring[s_o, 0:depth_o, pl.ds(pl.multiple_of(2 * piece * c, 2 * piece), 2 * piece)])
 
-    sent = all_sum(0, product_o, resid, ((0,), (1, 2), (3,), (4,)))
-    ld_tile(s_o).start()
+    sent = all_sum(0, product_o, resid, ((0,), (1, 2), (3,), (4,)), (s_o,))
     norm_chunks(gath.at[0], gain2, bias2, normed)
 
     for c in ld_up:
@@ -233,9 +237,7 @@
         cols = pl.ds(pl.multiple_of(2 * piece * c, 2 * piece), 2 * piece)
         return dotf(act[:, :ROWS], ring[s_down, :, cols]) + dotf(act[:, ROWS:], ring[s_down + 1, :, cols])
 
-    sent += all_sum(1, product_down, gath.at[0, me], ((5,), (6, 7, 8), (9, 10), (11,)))
-    ld_tile(s_down).start()
-    ld_tile(s_down + 1).start()
+    sent += all_sum(1, product_down, gath.at[0, me], ((5,), (6, 7, 8), (9, 10), (11, 12)), (s_down, s_down + 1))
     norm_chunks(gath.at[1], gainf, biasf, normed)
     for j in range(ways):
         y_out[:, j * piece:(j + 1) * piece] = gath[1, j]
@@ -271,25 +273,40 @@
             refill(2 * pair + t)
         return carry
 
-    def step(tile, carry):
-        slot = lax.rem(tile, RING)
-        ld_tile(tile).wait()
-        carry = reduce_tile(logits[rows_of(tile - 1)], carry)
-        logits[rows_of(tile)] = dotf(ring[slot], normed_t[...])
-        refill(tile)
+    def turned_product(tile):
+        for a in range(0, ROWS, BLOCK):
+            z = jnp.zeros((rows, BLOCK), F32)
+            for b in range(0, width, BLOCK):
+                z = z + dotf(normed[:, b:b + BLOCK], turned[a:a + BLOCK, b:b + BLOCK])
+            logits[pl.ds(pl.multiple_of(tile * ROWS + a, BLOCK), BLOCK)] = z.T
+
+    def step_pair(pair, carry):
+        tile = FLIPS + 2 * pair
+        plain, coming = lax.rem(tile + 1, RING), lax.rem(tile + 2, RING)
+        ld_tile(tile + 1).wait()
+        ld_tile(tile + 2).wait()
+        for t in range(2):
+            carry = reduce_tile(logits[rows_of(tile - 2 + t)], carry)
+        turned_product(tile)
+        for a in range(0, ROWS, BLOCK):
+            logits[pl.ds(pl.multiple_of((tile + 1) * ROWS + a, BLOCK), BLOCK)] = dotf(ring[plain, a:a + BLOCK], normed_t[...])
+            for b in range(width // ROWS * a, width // ROWS * (a + BLOCK), BLOCK):
+                for r in range(0, ROWS, BLOCK):
+                    turned[r:r + BLOCK, b:b + BLOCK] = ring[coming, r:r + BLOCK, b:b + BLOCK].T
+        refill(tile + 1)
+        refill(tile + 2)
         return carry
 
     logits[pl.ds(0, 2 * ROWS)] = jnp.full((2 * ROWS, rows), -1e30, F32)
     carry = (jnp.full((8, rows), -1e30, F32), jnp.zeros((8, rows), F32))
     carry = lax.fori_loop(0, FLIPS // 2, step_turned, carry)
-    last_turned = FLIPS // 2 * 2
-    carry = reduce_tile(logits[rows_of(last_turned - 2)], carry)
-    carry = lax.fori_loop(last_turned, n_full, step, carry)
+    carry = lax.fori_loop(0, (n_full - FLIPS - 1) // 2, step_pair, carry)
+    for t in range(n_full - 3, n_full - 1):
+        carry = reduce_tile(logits[rows_of(t)], carry)
     ld_last.wait()
-    carry = reduce_tile(logits[rows_of(n_full - 1)], carry)
-    z = dotf(last[...], normed_t[...])
-    logits[pl.ds(n_full * ROWS, rest)] = z
-    peak8, total8 = reduce_tile(z, carry)
+    turned_product(n_full - 1)
+    logits[pl.ds(n_full * ROWS, rest)] = dotf(last[...], normed_t[...])
+    peak8, total8 = reduce_tile(logits[pl.ds((n_full - 1) * ROWS, ROWS + rest)], carry)
     peak = jnp.max(peak8, axis=0, keepdims=True)
     total = jnp.sum(total8 * jnp.exp(peak8 - peak), axis=0, keepdims=True)
     row = lax.broadcasted_iota(jnp.int32, (8, rows), 0)
@@ -331,6 +348,7 @@
         out_specs=(vmem, vmem, vmem),
         scratch_shapes=[
             pltpu.VMEM((RING, ROWS, width), BF16),
+            pltpu.VMEM((ROWS, width), BF16),
             pltpu.VMEM((rest, width), BF16),
             pltpu.VMEM((rows, piece), BF16),
             pltpu.VMEM((rows, ff), BF16),

time: 90.4 us -> 85.6 us (0.947)
  Pallas kernels: 89.6 us -> 84.8 us
    pallas_call x1, Pallas kernels: 77.1 us -> 72.3 us  [run_tail(): pl.pallas_call(functools.partial(tail_kernel, ways), out_shape=(pltpu.VME...]
where the time goes in v4:
time: 85.6 us; the launch traced here: 85.4 us
  Pallas kernels  84.8 us (99%)
    pallas_call x1, Pallas kernels, run_tail(): pl.pallas_call(functools.partial(tail_kernel, ways), out_shape=(pltpu.VME...  72.3 us
    pallas_call x1, Pallas kernels, run_attend(): pl.pallas_call(attend_kernel, out_shape=(pltpu.VMEM((rows, q_cols), BF16)...  8.87 us
    pallas_call x1, Pallas kernels, run_finish(): pl.pallas_call(finish_kernel, out_shape=(jax.ShapeDtypeStruct((vocab, row...  3.58 us

profile of v4, /device:TPU:81, one launch (start us, length us, event | category | flops | bytes accessed | tf_op | source)
XLA Modules:
  0.0 85.4 jit_solution(3237499075933777274)
XLA Ops:
  0.6 8.9 %attend.1 = (bf16[128,384]{1,0:T(8,128)(2,1)S(1)}, bf16[128,64,128]{2,1,0:T(8,128)(2,1)}, bf16[128,64,128]{2,1,0:T(8,128)(2,1)}) custom-call(bf16[128,3072]{1,0:T(8,128)(2,1)} %hidden.3, s32[1,128]{1,0:T(1,128)} %bitcast.25, f32[1,3072]{1,0:T(1,128)} %bitcast.23, f32[1,3072]{1,0:T(1,128)} %bitcast.24, bf16[3072,384]{1,0:T(8,128)(2,1)} %w_q.1, ...), custom_call_target="tpu_custom_call" | custom-call | tf_op jit(solution)/shard_map/attend/pallas_call | solution.py:512
  9.5 72.3 %tail.1 = (f32[16032,128]{1,0:T(8,128)S(1)}, f32[8,128]{1,0:T(8,128)S(1)}, bf16[128,3072]{1,0:T(8,128)(2,1)S(1)}) custom-call(bf16[128,384]{1,0:T(8,128)(2,1)S(1)} %get-tuple-element.12.attended, bf16[128,3072]{1,0:T(8,128)(2,1)} %hidden.3, bf16[384,3072]{1,0:T(8,128)(2,1)} %w_o.1, bf16[3072,1024]{1,0:T(8,128)(2,1)} %w_up.1, bf16[1024,3072]{1,0:T(8,128)(2,1)} %w_down.1, ...), custom_call_target="tpu_custom_call" | custom-call | tf_op jit(solution)/shard_map/tail/pallas_call | solution.py:344
  81.8 3.6 %finish.1 = (f32[16032,128]{1,0:T(8,128)}, bf16[128,3072]{1,0:T(8,128)(2,1)}) custom-call(f32[16032,128]{1,0:T(8,128)S(1)} %get-tuple-element.13.logits, f32[8,128]{1,0:T(8,128)S(1)} %get-tuple-element.14.norm, bf16[128,3072]{1,0:T(8,128)(2,1)S(1)} %get-tuple-element.15.y), custom_call_target="tpu_custom_call" | custom-call | tf_op jit(solution)/shard_map/finish/pallas_call | solution.py:560

commit v5 on v4

--- a/solution.py
+++ b/solution.py
@@ -16,6 +16,10 @@
 RING = 13
 FLIPS = 12
 BLOCK = 256
+FILL = (
+    (((0, 1, 2), (0,)), (('up', 3), (1, 2)), (('down', 4, 5), (3,)), ((6, 7, 8), (4,))),
+    (((9, 10, 11, 12), (5,)), (('last',), (6, 7, 8)), ((), (9, 10)), ((), (11, 12))),
+)
 ROWS = 512
 NSEM = 26
 
@@ -85,15 +89,18 @@
 
     ld_o.start()
     ld_res.start()
-    for tile in range(4):
-        ld_tile(tile).start()
-    for c in ld_up:
-        c.start()
-    for c in ld_down:
-        c.start()
-    for tile in range(4, s_o):
-        ld_tile(tile).start()
-    ld_last.start()
+
+    def start(item):
+        if item == 'up':
+            for c in ld_up:
+                c.start()
+        elif item == 'down':
+            for c in ld_down:
+                c.start()
+        elif item == 'last':
+            ld_last.start()
+        else:
+            ld_tile(item).start()
 
     def flip(tile):
         ld_tile(tile).wait()
@@ -122,7 +129,13 @@
     def arrive(phase, idx, dst):
         copy(phase, idx, dst, dst, dev(chip, core)).wait_recv()
 
-    def all_sum(phase, product, residual, fill, freed):
+    def busy(work):
+        for item in work[0]:
+            start(item)
+        for tile in work[1]:
+            flip(tile)
+
+    def all_sum(phase, product, residual, fill):
         pb = parts.at[phase]
         sent = []
 
@@ -152,10 +165,7 @@
         go(copy(phase, 10, pb.at[2 * left + other, bot], sibh.at[phase, 1], dev(chip, other)))
         term(chip)
         go(copy(phase, 8, pb.at[2 * chip + other], sib.at[phase], dev(chip, other)))
-        for tile in freed:
-            ld_tile(tile).start()
-        for tile in fill[0]:
-            flip(tile)
+        busy(fill[0])
         for side, (to, rws) in enumerate(((right, top), (left, bot))):
             for k in range(2):
                 arrive(phase, 2 * side + k, raw1.at[phase, side, k])
@@ -163,8 +173,7 @@
             send3[phase, side] = (raw1[phase, side, 0].astype(F32) + raw1[phase, side, 1].astype(F32)
                                   + pb[2 * to + core, rws].astype(F32) + sibh[phase, side].astype(F32))
             go(copy(phase, 11 + side, send3.at[phase, side], recv3.at[phase, side], dev(to, core)))
-        for tile in fill[1]:
-            flip(tile)
+        busy(fill[1])
         arrive(phase, 8, sib.at[phase])
         for side, rws in enumerate((top, bot)):
             for k in range(2):
@@ -181,8 +190,7 @@
         go(copy(phase, 19, ob, g.at[me], dev(chip, other)))
         go(copy(phase, 14, ob.at[bot], g.at[me, bot], dev(right, core)))
         go(copy(phase, 15, ob.at[top], g.at[me, top], dev(left, core)))
-        for tile in fill[2]:
-            flip(tile)
+        busy(fill[2])
         ml, mr, mf = 2 * left + core, 2 * right + core, 2 * far + core
         arrive(phase, 13, g.at[ml, top])
         go(copy(phase, 17, g.at[ml, top], g.at[ml, top], dev(right, core)))
@@ -190,8 +198,7 @@
         go(copy(phase, 18, g.at[mr, bot], g.at[mr, bot], dev(left, core)))
         go(copy(phase, 20, g.at[ml, top], g.at[ml, top], dev(chip, other)))
         go(copy(phase, 21, g.at[mr, bot], g.at[mr, bot], dev(chip, other)))
-        for tile in fill[3]:
-            flip(tile)
+        busy(fill[3])
         arrive(phase, 14, g.at[ml, bot])
         go(copy(phase, 22, g.at[ml, bot], g.at[ml, bot], dev(chip, other)))
         arrive(phase, 15, g.at[mr, top])
@@ -217,7 +224,7 @@
     def product_o(c):
         return dotf(attended[...], ring[s_o, 0:depth_o, pl.ds(pl.multiple_of(2 * piece * c, 2 * piece), 2 * piece)])
 
-    sent = all_sum(0, product_o, resid, ((0,), (1, 2), (3,), (4,)), (s_o,))
+    sent = all_sum(0, product_o, resid, FILL[0])
     norm_chunks(gath.at[0], gain2, bias2, normed)
 
     for c in ld_up:
@@ -228,8 +235,6 @@
         for i in range(width // ROWS):
             total = total + dotf(normed[:, i * ROWS:(i + 1) * ROWS], ring[s_up + i // 3, :, (i % 3) * ff + n:(i % 3) * ff + n + 256])
         act[:, n:n + 256] = jnp.square(jnp.maximum(total, 0.0)).astype(BF16)
-    ld_tile(s_up).start()
-    ld_tile(s_up + 1).start()
     for c in ld_down:
         c.wait()
 
@@ -237,7 +242,7 @@
         cols = pl.ds(pl.multiple_of(2 * piece * c, 2 * piece), 2 * piece)
         return dotf(act[:, :ROWS], ring[s_down, :, cols]) + dotf(act[:, ROWS:], ring[s_down + 1, :, cols])
 
-    sent += all_sum(1, product_down, gath.at[0, me], ((5,), (6, 7, 8), (9, 10), (11, 12)), (s_down, s_down + 1))
+    sent += all_sum(1, product_down, gath.at[0, me], FILL[1])
     norm_chunks(gath.at[1], gainf, biasf, normed)
     for j in range(ways):
         y_out[:, j * piece:(j + 1) * piece] = gath[1, j]

time: 85.6 us -> 83 us (0.970)
  Pallas kernels: 84.8 us -> 82.2 us
    pallas_call x1, Pallas kernels: 72.3 us -> 69.7 us  [run_tail(): pl.pallas_call(functools.partial(tail_kernel, ways), out_shape=(pltpu.VME...]
where the time goes in v5:
time: 83 us; the launch traced here: 82.8 us
  Pallas kernels  82.2 us (99%)
    pallas_call x1, Pallas kernels, run_tail(): pl.pallas_call(functools.partial(tail_kernel, ways), out_shape=(pltpu.VME...  69.7 us
    pallas_call x1, Pallas kernels, run_attend(): pl.pallas_call(attend_kernel, out_shape=(pltpu.VMEM((rows, q_cols), BF16)...  8.87 us
    pallas_call x1, Pallas kernels, run_finish(): pl.pallas_call(finish_kernel, out_shape=(jax.ShapeDtypeStruct((vocab, row...  3.58 us

profile of v5, /device:TPU:81, one launch (start us, length us, event | category | flops | bytes accessed | tf_op | source)
XLA Modules:
  0.0 82.8 jit_solution(4260821623941023778)
XLA Ops:
  0.6 8.9 %attend.1 = (bf16[128,384]{1,0:T(8,128)(2,1)S(1)}, bf16[128,64,128]{2,1,0:T(8,128)(2,1)}, bf16[128,64,128]{2,1,0:T(8,128)(2,1)}) custom-call(bf16[128,3072]{1,0:T(8,128)(2,1)} %hidden.3, s32[1,128]{1,0:T(1,128)} %bitcast.25, f32[1,3072]{1,0:T(1,128)} %bitcast.23, f32[1,3072]{1,0:T(1,128)} %bitcast.24, bf16[3072,384]{1,0:T(8,128)(2,1)} %w_q.1, ...), custom_call_target="tpu_custom_call" | custom-call | tf_op jit(solution)/shard_map/attend/pallas_call | solution.py:517
  9.5 69.7 %tail.1 = (f32[16032,128]{1,0:T(8,128)S(1)}, f32[8,128]{1,0:T(8,128)S(1)}, bf16[128,3072]{1,0:T(8,128)(2,1)S(1)}) custom-call(bf16[128,384]{1,0:T(8,128)(2,1)S(1)} %get-tuple-element.12.attended, bf16[128,3072]{1,0:T(8,128)(2,1)} %hidden.3, bf16[384,3072]{1,0:T(8,128)(2,1)} %w_o.1, bf16[3072,1024]{1,0:T(8,128)(2,1)} %w_up.1, bf16[1024,3072]{1,0:T(8,128)(2,1)} %w_down.1, ...), custom_call_target="tpu_custom_call" | custom-call | tf_op jit(solution)/shard_map/tail/pallas_call | solution.py:349
  79.2 3.6 %finish.1 = (f32[16032,128]{1,0:T(8,128)}, bf16[128,3072]{1,0:T(8,128)(2,1)}) custom-call(f32[16032,128]{1,0:T(8,128)S(1)} %get-tuple-element.13.logits, f32[8,128]{1,0:T(8,128)S(1)} %get-tuple-element.14.norm, bf16[128,3072]{1,0:T(8,128)(2,1)S(1)} %get-tuple-element.15.y), custom_call_target="tpu_custom_call" | custom-call | tf_op jit(solution)/shard_map/finish/pallas_call | solution.py:565

commit v6 on v5

--- a/solution.py
+++ b/solution.py
@@ -16,8 +16,9 @@
 RING = 13
 FLIPS = 12
 BLOCK = 256
+QUAD = 4
 FILL = (
-    (((0, 1, 2), (0,)), (('up', 3), (1, 2)), (('down', 4, 5), (3,)), ((6, 7, 8), (4,))),
+    (((0, 1, 2, 3), (0,)), (('up',), (1, 2)), (('down', 4, 5), (3,)), ((6, 7, 8), (4,))),
     (((9, 10, 11, 12), (5,)), (('last',), (6, 7, 8)), ((), (9, 10)), ((), (11, 12))),
 )
 ROWS = 512
@@ -70,13 +71,12 @@
     vocab, width = w_out.shape
     n_full = vocab // ROWS
     rest = vocab - n_full * ROWS
-    s_o, s_up, s_down = RING - 5, RING - 4, RING - 2
+    s_up, s_down = RING - 4, RING - 2
 
     def dev(c, k):
         return {'tp': 2 * c + k}
 
     ld_res = pltpu.make_async_copy(hidden.at[:, pl.ds(pl.multiple_of(me * piece, piece), piece)], resid, small_sem.at[0])
-    ld_o = pltpu.make_async_copy(w_o, ring.at[s_o, pl.ds(0, w_o.shape[0])], w_sem.at[s_o])
     ld_up = []
     for i in range(width // ROWS):
         ld_up.append(pltpu.make_async_copy(w_up.at[pl.ds(i * ROWS, ROWS)], ring.at[s_up + i // 3, :, pl.ds((i % 3) * w_up.shape[1], w_up.shape[1])], small_sem.at[4 + i]))
@@ -87,7 +87,6 @@
         slot = lax.rem(tile, RING)
         return pltpu.make_async_copy(w_out.at[pl.ds(pl.multiple_of(tile * ROWS, ROWS), ROWS)], ring.at[slot], w_sem.at[slot])
 
-    ld_o.start()
     ld_res.start()
 
     def start(item):
@@ -136,7 +135,7 @@
             flip(tile)
 
     def all_sum(phase, product, residual, fill):
-        pb = parts.at[phase]
+        pb = parts
         sent = []
 
         def go(c):
@@ -217,12 +216,10 @@
         arrive(phase, 25, g.at[of, bot])
         return sent
 
-    ld_o.wait()
     ld_res.wait()
-    depth_o = w_o.shape[0]
 
     def product_o(c):
-        return dotf(attended[...], ring[s_o, 0:depth_o, pl.ds(pl.multiple_of(2 * piece * c, 2 * piece), 2 * piece)])
+        return dotf(attended[...], w_o[:, pl.ds(pl.multiple_of(2 * piece * c, 2 * piece), 2 * piece)])
 
     sent = all_sum(0, product_o, resid, FILL[0])
     norm_chunks(gath.at[0], gain2, bias2, normed)
@@ -242,7 +239,9 @@
         cols = pl.ds(pl.multiple_of(2 * piece * c, 2 * piece), 2 * piece)
         return dotf(act[:, :ROWS], ring[s_down, :, cols]) + dotf(act[:, ROWS:], ring[s_down + 1, :, cols])
 
-    sent += all_sum(1, product_down, gath.at[0, me], FILL[1])
+    for c in sent:
+        c.wait_send()
+    sent = all_sum(1, product_down, gath.at[0, me], FILL[1])
     norm_chunks(gath.at[1], gainf, biasf, normed)
     for j in range(ways):
         y_out[:, j * piece:(j + 1) * piece] = gath[1, j]
@@ -263,19 +262,18 @@
         def _():
             ld_tile(tile + RING).start()
 
-    def step_turned(pair, carry):
-        for t in range(2):
-            before = jnp.maximum(2 * pair - 2 + t, 0)
-            carry = reduce_tile(logits[rows_of(before)], carry)
-        for t in range(2):
-            tile = 2 * pair + t
+    def step_turned(quad, carry):
+        for t in range(QUAD):
+            tile = QUAD * quad + t
+            carry = reduce_tile(logits[rows_of(jnp.maximum(tile - QUAD, 0))], carry)
+        for t in range(QUAD):
+            tile = QUAD * quad + t
             for a in range(0, ROWS, BLOCK):
                 z = jnp.zeros((rows, BLOCK), F32)
                 for b in range(0, width, BLOCK):
                     z = z + dotf(normed[:, b:b + BLOCK], ring[tile, a:a + BLOCK, b:b + BLOCK])
                 logits[pl.ds(pl.multiple_of(tile * ROWS + a, BLOCK), BLOCK)] = z.T
-        for t in range(2):
-            refill(2 * pair + t)
+            refill(tile)
         return carry
 
     def turned_product(tile):
@@ -302,9 +300,11 @@
         refill(tile + 2)
         return carry
 
-    logits[pl.ds(0, 2 * ROWS)] = jnp.full((2 * ROWS, rows), -1e30, F32)
+    logits[pl.ds(0, ROWS)] = jnp.full((ROWS, rows), -1e30, F32)
     carry = (jnp.full((8, rows), -1e30, F32), jnp.zeros((8, rows), F32))
-    carry = lax.fori_loop(0, FLIPS // 2, step_turned, carry)
+    carry = lax.fori_loop(0, FLIPS // QUAD, step_turned, carry)
+    for t in range(FLIPS - QUAD, FLIPS - 2):
+        carry = reduce_tile(logits[rows_of(t)], carry)
     carry = lax.fori_loop(0, (n_full - FLIPS - 1) // 2, step_pair, carry)
     for t in range(n_full - 3, n_full - 1):
         carry = reduce_tile(logits[rows_of(t)], carry)
@@ -349,7 +349,7 @@
     return pl.pallas_call(
         functools.partial(tail_kernel, ways),
         out_shape=(pltpu.VMEM((vocab, rows), F32), pltpu.VMEM((8, rows), F32), pltpu.VMEM((rows, width), BF16)),
-        in_specs=[vmem, hbm, hbm, hbm, hbm, hbm, vmem, vmem, vmem, vmem],
+        in_specs=[vmem, hbm, vmem, hbm, hbm, hbm, vmem, vmem, vmem, vmem],
         out_specs=(vmem, vmem, vmem),
         scratch_shapes=[
             pltpu.VMEM((RING, ROWS, width), BF16),
@@ -359,7 +359,7 @@
             pltpu.VMEM((rows, ff), BF16),
             pltpu.VMEM((rows, width), BF16),
             pltpu.VMEM((width, rows), BF16),
-            pltpu.VMEM((2, ways, rows, piece), BF16),
+            pltpu.VMEM((ways, rows, piece), BF16),
             pltpu.VMEM((2, 2, 2, half, piece), BF16),
             pltpu.VMEM((2, 2, 2, half, piece), BF16),
             pltpu.VMEM((2, rows, piece), BF16),
@@ -378,18 +378,18 @@
         ],
         compiler_params=pltpu.CompilerParams(collective_id=0, has_side_effects=True, vmem_limit_bytes=LIMIT),
         name='tail',
-    )(pltpu.with_memory_space_constraint(attended, pltpu.VMEM), hidden, w_o, w_up, w_down, w_out_t, gain2, bias2, gainf, biasf)
-
-
-LIMIT = 53 * 1024 * 1024
+    )(pltpu.with_memory_space_constraint(attended, pltpu.VMEM), hidden, pltpu.with_memory_space_constraint(w_o, pltpu.VMEM), w_up, w_down, w_out_t, gain2, bias2, gainf, biasf)
+
+
+LIMIT = int(51.6 * 1024 * 1024)
 
 
 CHUNKS = 4
 PROJ = 2
 
 
-def attend_kernel(hidden, lengths, gain, bias, w_q, w_k, w_v, cache_k, cache_v,
-                  attended, out_k, out_v,
+def attend_kernel(hidden, lengths, gain, bias, w_q, w_k, w_v, w_o, cache_k, cache_v,
+                  attended, o_out, out_k, out_v,
                   x, gb, len_row, normed, w_qkv, qkv, len_col, k_buf, v_buf, misc_sem, w_sem, in_sem, out_sem):
     rows, width = hidden.shape
     seqs, slots, dim = cache_k.shape
@@ -422,6 +422,8 @@
         for c in kv_in[-1]:
             c.start()
 
+    ld_o = pltpu.make_async_copy(w_o, o_out, misc_sem.at[4])
+    ld_o.start()
     small[3].wait()
     lens = jnp.broadcast_to(len_row[...].astype(F32), (rows, rows)).T
     len_col[...] = lens
@@ -485,6 +487,7 @@
         lax.fori_loop(0, step_s // 8, put, 0)
         for c in kv_out[i]:
             c.start()
+    for i in range(CHUNKS):
         groups = [i * step_s + g * group for g in range(step_s // group)]
         all_scores = []
         for b in groups:
@@ -506,9 +509,10 @@
     for pair in kv_out:
         for c in pair:
             c.wait()
-
-
-def run_attend(hidden, cache_k, cache_v, lengths, gain, bias, w_q, w_k, w_v):
+    ld_o.wait()
+
+
+def run_attend(hidden, cache_k, cache_v, lengths, gain, bias, w_q, w_k, w_v, w_o):
     rows, width = hidden.shape
     seqs, slots, dim = cache_k.shape
     q_cols = w_q.shape[1]
@@ -516,9 +520,9 @@
     vmem = pl.BlockSpec(memory_space=pltpu.VMEM)
     return pl.pallas_call(
         attend_kernel,
-        out_shape=(pltpu.VMEM((rows, q_cols), BF16), jax.ShapeDtypeStruct(cache_k.shape, BF16), jax.ShapeDtypeStruct(cache_v.shape, BF16)),
-        in_specs=[hbm] * 9,
-        out_specs=(vmem, hbm, hbm),
+        out_shape=(pltpu.VMEM((rows, q_cols), BF16), pltpu.VMEM(w_o.shape, BF16), jax.ShapeDtypeStruct(cache_k.shape, BF16), jax.ShapeDtypeStruct(cache_v.shape, BF16)),
+        in_specs=[hbm] * 10,
+        out_specs=(vmem, vmem, hbm, hbm),
         scratch_shapes=[
             pltpu.VMEM((rows, width), BF16),
             pltpu.VMEM((8, width), F32),
@@ -529,14 +533,14 @@
             pltpu.VMEM((rows, rows), F32),
             pltpu.VMEM((seqs, slots, dim), BF16),
             pltpu.VMEM((seqs, slots, dim), BF16),
-            pltpu.SemaphoreType.DMA((4,)),
+            pltpu.SemaphoreType.DMA((5,)),
             pltpu.SemaphoreType.DMA((3, PROJ)),
             pltpu.SemaphoreType.DMA((2, CHUNKS)),
             pltpu.SemaphoreType.DMA((2, CHUNKS)),
         ],
-        compiler_params=pltpu.CompilerParams(vmem_limit_bytes=62 * 1024 * 1024),
+        compiler_params=pltpu.CompilerParams(vmem_limit_bytes=40 * 1024 * 1024),
         name='attend',
-    )(hidden, lengths, gain, bias, w_q, w_k, w_v, cache_k, cache_v)
+    )(*(pltpu.with_memory_space_constraint(v, pltpu.HBM) for v in (hidden, lengths, gain, bias, w_q, w_k, w_v, w_o, cache_k, cache_v)))
 
 
 PARTS = 8
@@ -585,7 +589,7 @@
     def local_step(new_hidden, cache_k, cache_v, lengths, ln1_gain, ln1_bias, w_q, w_k, w_v, w_o, ln2_gain, ln2_bias, w_up, w_down, lnf_gain, lnf_bias, w_out):
         shape = cache_k.shape
         flat = (shape[0], shape[1], shape[3])
-        attended, new_cache_k, new_cache_v = run_attend(new_hidden, cache_k.reshape(flat), cache_v.reshape(flat), lengths[None], ln1_gain[None], ln1_bias[None], w_q, w_k, w_v)
+        attended, w_o, new_cache_k, new_cache_v = run_attend(new_hidden, cache_k.reshape(flat), cache_v.reshape(flat), lengths[None], ln1_gain[None], ln1_bias[None], w_q, w_k, w_v, w_o)
         logits, norm, y = run_tail(ways, attended, new_hidden, w_o, w_up, w_down, w_out.T,
                                    ln2_gain[None], ln2_bias[None], lnf_gain[None], lnf_bias[None])
         log_probs_t, out_hidden = run_finish(logits, norm, y)

time: 83 us -> 81.6 us (0.983)
  Pallas kernels: 82.2 us -> 80.6 us
    pallas_call x1, Pallas kernels: 8.87 us -> 7.95 us  [run_attend(): pl.pallas_call(attend_kernel, out_shape=(pltpu.VMEM((rows, q_cols), BF16)...]
where the time goes in v6:
time: 81.6 us; the launch traced here: 81.4 us
  Pallas kernels  80.6 us (99%)
    pallas_call x1, Pallas kernels, run_tail(): pl.pallas_call(functools.partial(tail_kernel, ways), out_shape=(pltpu.VME...  69.1 us
    pallas_call x1, Pallas kernels, run_attend(): pl.pallas_call(attend_kernel, out_shape=(pltpu.VMEM((rows, q_cols), BF16)...  7.95 us
    pallas_call x1, Pallas kernels, run_finish(): pl.pallas_call(finish_kernel, out_shape=(jax.ShapeDtypeStruct((vocab, row...  3.58 us

profile of v6, /device:TPU:81, one launch (start us, length us, event | category | flops | bytes accessed | tf_op | source)
XLA Modules:
  0.0 81.4 jit_solution(8760277293628911442)
XLA Ops:
  0.6 8.0 %attend.1 = (bf16[128,384]{1,0:T(8,128)(2,1)S(1)}, bf16[384,3072]{1,0:T(8,128)(2,1)S(1)}, bf16[128,64,128]{2,1,0:T(8,128)(2,1)}, bf16[128,64,128]{2,1,0:T(8,128)(2,1)}) custom-call(bf16[128,3072]{1,0:T(8,128)(2,1)} %hidden.3, s32[1,128]{1,0:T(1,128)} %bitcast.25, f32[1,3072]{1,0:T(1,128)} %bitcast.23, f32[1,3072]{1,0:T(1,128)} %bitcast.24, ...), custom_call_target="tpu_custom_call" | custom-call | tf_op jit(solution)/shard_map/attend/pallas_call | solution.py:521
  8.6 69.1 %tail.1 = (f32[16032,128]{1,0:T(8,128)S(1)}, f32[8,128]{1,0:T(8,128)S(1)}, bf16[128,3072]{1,0:T(8,128)(2,1)S(1)}) custom-call(bf16[128,384]{1,0:T(8,128)(2,1)S(1)} %get-tuple-element.13.attended, bf16[128,3072]{1,0:T(8,128)(2,1)} %hidden.3, bf16[384,3072]{1,0:T(8,128)(2,1)S(1)} %get-tuple-element.14.w_o, bf16[3072,1024]{1,0:T(8,128)(2,1)} %w_up.1, ...), custom_call_target="tpu_custom_call" | custom-call | tf_op jit(solution)/shard_map/tail/pallas_call | solution.py:349
  77.7 3.6 %finish.1 = (f32[16032,128]{1,0:T(8,128)}, bf16[128,3072]{1,0:T(8,128)(2,1)}) custom-call(f32[16032,128]{1,0:T(8,128)S(1)} %get-tuple-element.15.logits, f32[8,128]{1,0:T(8,128)S(1)} %get-tuple-element.16.norm, bf16[128,3072]{1,0:T(8,128)(2,1)S(1)} %get-tuple-element.17.y), custom_call_target="tpu_custom_call" | custom-call | tf_op jit(solution)/shard_map/finish/pallas_call | solution.py:569

commit v7 on v6

--- a/solution.py
+++ b/solution.py
@@ -18,8 +18,8 @@
 BLOCK = 256
 QUAD = 4
 FILL = (
-    (((0, 1, 2, 3), (0,)), (('up',), (1, 2)), (('down', 4, 5), (3,)), ((6, 7, 8), (4,))),
-    (((9, 10, 11, 12), (5,)), (('last',), (6, 7, 8)), ((), (9, 10)), ((), (11, 12))),
+    (((2, 3), (0,)), ((4, 'up'), (1, 2)), ((5, 'down'), (3,)), ((6, 7, 8), (4,))),
+    (((9, 10), (5,)), ((11, 12), (6, 7, 8)), (('last',), (9, 10)), ((), (11, 12))),
 )
 ROWS = 512
 NSEM = 26
@@ -116,6 +116,8 @@
         if tile == FLIPS:
             ld_tile(tile + RING).start()
 
+    start(0)
+    start(1)
     barrier = pltpu.get_barrier_semaphore()
     for d in range(1, ways):
         pl.semaphore_signal(barrier, inc=1, device_id={'tp': lax.rem(me + d, ways)}, device_id_type=MESH)
@@ -273,7 +275,7 @@
                 for b in range(0, width, BLOCK):
                     z = z + dotf(normed[:, b:b + BLOCK], ring[tile, a:a + BLOCK, b:b + BLOCK])
                 logits[pl.ds(pl.multiple_of(tile * ROWS + a, BLOCK), BLOCK)] = z.T
-            refill(tile)
+            ld_tile(tile + RING).start()
         return carry
 
     def turned_product(tile):

time: 81.6 us -> 83.5 us (1.023)
  Pallas kernels: 80.6 us -> 82.5 us
    pallas_call x1, Pallas kernels: 69.1 us -> 71 us  [run_tail(): pl.pallas_call(functools.partial(tail_kernel, ways), out_shape=(pltpu.VME...]
where the time goes in v7:
time: 83.5 us; the launch traced here: 83.3 us
  Pallas kernels  82.5 us (99%)
    pallas_call x1, Pallas kernels, run_tail(): pl.pallas_call(functools.partial(tail_kernel, ways), out_shape=(pltpu.VME...  71 us
    pallas_call x1, Pallas kernels, run_attend(): pl.pallas_call(attend_kernel, out_shape=(pltpu.VMEM((rows, q_cols), BF16)...  7.95 us
    pallas_call x1, Pallas kernels, run_finish(): pl.pallas_call(finish_kernel, out_shape=(jax.ShapeDtypeStruct((vocab, row...  3.58 us

profile of v7, /device:TPU:81, one launch (start us, length us, event | category | flops | bytes accessed | tf_op | source)
XLA Modules:
  0.0 83.3 jit_solution(16224398186993327877)
XLA Ops:
  0.6 8.0 %attend.1 = (bf16[128,384]{1,0:T(8,128)(2,1)S(1)}, bf16[384,3072]{1,0:T(8,128)(2,1)S(1)}, bf16[128,64,128]{2,1,0:T(8,128)(2,1)}, bf16[128,64,128]{2,1,0:T(8,128)(2,1)}) custom-call(bf16[128,3072]{1,0:T(8,128)(2,1)} %hidden.3, s32[1,128]{1,0:T(1,128)} %bitcast.25, f32[1,3072]{1,0:T(1,128)} %bitcast.23, f32[1,3072]{1,0:T(1,128)} %bitcast.24, ...), custom_call_target="tpu_custom_call" | custom-call | tf_op jit(solution)/shard_map/attend/pallas_call | solution.py:523
  8.6 71.0 %tail.1 = (f32[16032,128]{1,0:T(8,128)S(1)}, f32[8,128]{1,0:T(8,128)S(1)}, bf16[128,3072]{1,0:T(8,128)(2,1)S(1)}) custom-call(bf16[128,384]{1,0:T(8,128)(2,1)S(1)} %get-tuple-element.13.attended, bf16[128,3072]{1,0:T(8,128)(2,1)} %hidden.3, bf16[384,3072]{1,0:T(8,128)(2,1)S(1)} %get-tuple-element.14.w_o, bf16[3072,1024]{1,0:T(8,128)(2,1)} %w_up.1, ...), custom_call_target="tpu_custom_call" | custom-call | tf_op jit(solution)/shard_map/tail/pallas_call | solution.py:351
  79.6 3.6 %finish.1 = (f32[16032,128]{1,0:T(8,128)}, bf16[128,3072]{1,0:T(8,128)(2,1)}) custom-call(f32[16032,128]{1,0:T(8,128)S(1)} %get-tuple-element.15.logits, f32[8,128]{1,0:T(8,128)S(1)} %get-tuple-element.16.norm, bf16[128,3072]{1,0:T(8,128)(2,1)S(1)} %get-tuple-element.17.y), custom_call_target="tpu_custom_call" | custom-call | tf_op jit(solution)/shard_map/finish/pallas_call | solution.py:571

commit v8 on v7

--- a/solution.py
+++ b/solution.py
@@ -18,8 +18,8 @@
 BLOCK = 256
 QUAD = 4
 FILL = (
-    (((2, 3), (0,)), ((4, 'up'), (1, 2)), ((5, 'down'), (3,)), ((6, 7, 8), (4,))),
-    (((9, 10), (5,)), ((11, 12), (6, 7, 8)), (('last',), (9, 10)), ((), (11, 12))),
+    (((0, 1), ()), (('up', 2, 3), (0, 1)), ((4, 5, 6), (2, 3)), ((), (4,)), (('down',), ())),
+    (((7, 8), (5, 6)), ((9, 10, 11, 12), (7, 8)), ((), (9, 10)), ((), (11, 12)), ((FLIPS + RING, 'last'), ())),
 )
 ROWS = 512
 NSEM = 26
@@ -113,11 +113,7 @@
             return carry
 
         lax.fori_loop(0, width // BLOCK // 2, turn, 0)
-        if tile == FLIPS:
-            ld_tile(tile + RING).start()
-
-    start(0)
-    start(1)
+
     barrier = pltpu.get_barrier_semaphore()
     for d in range(1, ways):
         pl.semaphore_signal(barrier, inc=1, device_id={'tp': lax.rem(me + d, ways)}, device_id_type=MESH)
@@ -208,6 +204,7 @@
         go(copy(phase, 24, g.at[mf, top], g.at[mf, top], dev(chip, other)))
         arrive(phase, 18, g.at[mf, bot])
         go(copy(phase, 25, g.at[mf, bot], g.at[mf, bot], dev(chip, other)))
+        busy(fill[4])
         ol, orr, of = 2 * left + other, 2 * right + other, 2 * far + other
         arrive(phase, 19, g.at[2 * chip + other])
         arrive(phase, 20, g.at[ol, top])

time: 83.5 us -> 82.5 us (0.988)
  Pallas kernels: 82.5 us -> 81.4 us
    pallas_call x1, Pallas kernels: 71 us -> 69.9 us  [run_tail(): pl.pallas_call(functools.partial(tail_kernel, ways), out_shape=(pltpu.VME...]
where the time goes in v8:
time: 82.5 us; the launch traced here: 82.3 us
  Pallas kernels  81.4 us (99%)
    pallas_call x1, Pallas kernels, run_tail(): pl.pallas_call(functools.partial(tail_kernel, ways), out_shape=(pltpu.VME...  69.9 us
    pallas_call x1, Pallas kernels, run_attend(): pl.pallas_call(attend_kernel, out_shape=(pltpu.VMEM((rows, q_cols), BF16)...  7.95 us
    pallas_call x1, Pallas kernels, run_finish(): pl.pallas_call(finish_kernel, out_shape=(jax.ShapeDtypeStruct((vocab, row...  3.58 us

profile of v8, /device:TPU:81, one launch (start us, length us, event | category | flops | bytes accessed | tf_op | source)
XLA Modules:
  0.0 82.3 jit_solution(5407602648239429040)
XLA Ops:
  0.6 8.0 %attend.1 = (bf16[128,384]{1,0:T(8,128)(2,1)S(1)}, bf16[384,3072]{1,0:T(8,128)(2,1)S(1)}, bf16[128,64,128]{2,1,0:T(8,128)(2,1)}, bf16[128,64,128]{2,1,0:T(8,128)(2,1)}) custom-call(bf16[128,3072]{1,0:T(8,128)(2,1)} %hidden.3, s32[1,128]{1,0:T(1,128)} %bitcast.25, f32[1,3072]{1,0:T(1,128)} %bitcast.23, f32[1,3072]{1,0:T(1,128)} %bitcast.24, ...), custom_call_target="tpu_custom_call" | custom-call | tf_op jit(solution)/shard_map/attend/pallas_call | solution.py:520
  8.6 69.9 %tail.1 = (f32[16032,128]{1,0:T(8,128)S(1)}, f32[8,128]{1,0:T(8,128)S(1)}, bf16[128,3072]{1,0:T(8,128)(2,1)S(1)}) custom-call(bf16[128,384]{1,0:T(8,128)(2,1)S(1)} %get-tuple-element.13.attended, bf16[128,3072]{1,0:T(8,128)(2,1)} %hidden.3, bf16[384,3072]{1,0:T(8,128)(2,1)S(1)} %get-tuple-element.14.w_o, bf16[3072,1024]{1,0:T(8,128)(2,1)} %w_up.1, ...), custom_call_target="tpu_custom_call" | custom-call | tf_op jit(solution)/shard_map/tail/pallas_call | solution.py:348
  78.5 3.6 %finish.1 = (f32[16032,128]{1,0:T(8,128)}, bf16[128,3072]{1,0:T(8,128)(2,1)}) custom-call(f32[16032,128]{1,0:T(8,128)S(1)} %get-tuple-element.15.logits, f32[8,128]{1,0:T(8,128)S(1)} %get-tuple-element.16.norm, bf16[128,3072]{1,0:T(8,128)(2,1)S(1)} %get-tuple-element.17.y), custom_call_target="tpu_custom_call" | custom-call | tf_op jit(solution)/shard_map/finish/pallas_call | solution.py:568
